TPU v7x, 32 devices: a whole 2x2x4 slice. The times are simulated.
32 devices in a mesh: section: 4 (over z), batch: 2 (over x), tile: 4 (over y, core).
Axes of the slice: x: 2, y: 2, z: 4, core: 2. Of those that a mesh axis runs over, the one named last changes fastest.
Arguments:
- latents: bfloat16 [8, 4, 32, 1280], P('batch', 'tile'), parts along dimension 0, may hold values from -6 to 6
- prompt_tokens: bfloat16 [8, 77, 2048], P('batch'), parts along dimension 0, may hold values from -6 to 6
- fresh_noise: bfloat16 [1, 8, 4, 32, 1280], P(None, 'batch', 'tile'), parts along dimension 1, may hold values from -6 to 6
- timesteps: int32 [2], replicated, may hold values from 600 to 999
- entry_order: int32 [8], P('batch'), parts along dimension 0, may hold values from 0 to 3, each once
- timestep_weight: bfloat16 [4, 320, 1280], P('section'), may hold values from -0.3125 to 0.3125
- conv_kernel: float32 [4, 9, 1280], P('section'), may hold values from -1 to 1
- norm_gain: float32 [4, 1280], P('section'), may hold values from 0.25 to 1.75
- layer_norm_bias: float32 [4, 1280], P('section'), may hold values from -1.5 to 1.5
- qkv_weight: bfloat16 [4, 1280, 3, 1280], P('section', None, None, 'tile'), may hold values from -0.15625 to 0.15625
- prompt_weight: bfloat16 [4, 2048, 2, 1280], P('section', None, None, 'tile'), may hold values from -0.125 to 0.125
- out_weight: bfloat16 [4, 1280, 1280], P('section', 'tile'), may hold values from -0.15625 to 0.15625
Outputs:
- samples: bfloat16 [8, 4, 32, 1280], P('batch', 'tile', None, 'section'), parts along dimension 0
There are 2 independent parts, one for each index of `batch`. A program takes and returns all parts, laid end to end along the dimension named above; an argument that names none is the same for every part. Nothing has to cross between parts.
All inputs are finite; a program needn't handle non-finite values.
Results may differ from a plain program's by a relative error of at most 0.019.
Values may be sent and summed in bfloat16 or wider, within the bound.
No kernel may reach another device: no remote copies, remote signals or barrier semaphores. Data moves between devices by JAX's collectives and lax.ppermute only.
A program may use at most 64 MiB of HBM per device.

v0:
```python
import functools
import math

import jax
import jax.numpy as jnp
from jax import lax
from jax.experimental import pallas as pl
from jax.experimental.pallas import tpu as pltpu
from jax.sharding import PartitionSpec as P


HEADS = 20
LANES = 128


def alpha_bar_at(position):
    shape = (8, LANES)
    positions = lax.broadcasted_iota(jnp.int32, shape, 0) * LANES
    positions = positions + lax.broadcasted_iota(jnp.int32, shape, 1)
    low_root = math.sqrt(0.00085)
    high_root = math.sqrt(0.012)
    roots = low_root + (high_root - low_root) * positions.astype(jnp.float32) / 999.0
    logs = jnp.where(positions <= position, jnp.log(1.0 - roots * roots), 0.0)
    return jnp.exp(jnp.sum(jnp.sum(logs, axis=1, keepdims=True), axis=0, keepdims=True))


def time_features(timesteps, half_count):
    exponents = jnp.arange(half_count, dtype=jnp.float32) / half_count
    freq_row = jnp.exp(-math.log(10000.0) * exponents)
    angles = timesteps.astype(jnp.float32)[:, None] * freq_row[None, :]
    return jnp.concatenate([jnp.cos(angles), jnp.sin(angles)], axis=1).astype(jnp.bfloat16)


def swapped(value, axis, mask):
    count = lax.axis_size(axis)
    return lax.ppermute(value, axis, [(i, i ^ mask) for i in range(count)])


def prompt_kernel(token_ref, weight_ref, out_ref):
    slots = token_ref.shape[1]
    rows = lax.dot_general(
        weight_ref[...],
        token_ref[...].reshape(2 * slots, token_ref.shape[2]),
        (((1,), (1,)), ((), ())),
        preferred_element_type=jnp.float32,
    ).astype(jnp.bfloat16)
    out_ref[0] = rows[:, :slots]
    out_ref[1] = rows[:, slots:]


def project_prompts(tokens, weight):
    count, slots, width = tokens.shape
    rows = weight.shape[0]
    return pl.pallas_call(
        prompt_kernel,
        grid=(count // 2,),
        in_specs=[
            pl.BlockSpec((2, slots, width), lambda i: (i, 0, 0)),
            pl.BlockSpec((rows, width), lambda i: (0, 0)),
        ],
        out_specs=pl.BlockSpec((2, rows, slots), lambda i: (i, 0, 0)),
        out_shape=jax.ShapeDtypeStruct((count, rows, slots), jnp.bfloat16),
        compiler_params=pltpu.CompilerParams(vmem_limit_bytes=60 * 2**20),
        name="prompts",
    )(tokens, weight)


def pick_kernel(masks, block, flag_ref, order_ref, source_ref, *refs):
    outs, sems = refs[:-1], refs[-1]
    tile = flag_ref[1]
    copies = []
    for index, out in enumerate(outs):
        for j, mask in enumerate(masks[index]):
            entry = tile ^ mask
            if order_ref is not None:
                wanted = entry
                entry = jnp.int32(0)
                for m in range(order_ref.shape[0]):
                    entry = entry + jnp.where(order_ref[m] == wanted, m, 0)
            rows = pl.ds(pl.multiple_of(entry * block, 16), block)
            copies.append(
                pltpu.make_async_copy(source_ref.at[rows], out.at[j], sems.at[index, j])
            )
    for copy in copies:
        copy.start()
    for copy in copies:
        copy.wait()


def pick(flags, order, source, block, masks, vmem_total):
    kernel = functools.partial(pick_kernel, masks, block)
    if order is None:
        kernel = lambda flag_ref, *refs: pick_kernel(masks, block, flag_ref, None, *refs)
    smem = pl.BlockSpec(memory_space=pltpu.SMEM)
    width = source.shape[1]
    return pl.pallas_call(
        kernel,
        in_specs=[smem] + ([smem] if order is not None else []) + [pl.BlockSpec(memory_space=pltpu.HBM)],
        out_specs=[pl.BlockSpec(memory_space=pltpu.VMEM)] * len(masks),
        out_shape=[jax.ShapeDtypeStruct((len(m), block, width), source.dtype) for m in masks],
        scratch_shapes=[pltpu.SemaphoreType.DMA((len(masks), len(masks[0])))],
        compiler_params=pltpu.CompilerParams(vmem_limit_bytes=vmem_total * 2**20),
    )(flags, *([order] if order is not None else []), source)


def cut_kernel(which, flag_ref, qkv_ref, last_ref, *refs):
    outs, sems = refs[:-1], refs[-1]
    half = outs[0].shape[0]
    parity = flag_ref[2] if which == 0 else 1 - flag_ref[2]
    rows = pl.ds(pl.multiple_of(parity * half, 16), half)
    copies = []
    for piece, out in enumerate(outs):
        source = qkv_ref.at[piece, rows] if piece < 3 else last_ref.at[rows]
        copies.append(pltpu.make_async_copy(source, out, sems.at[piece]))
    for copy in copies:
        copy.start()
    for copy in copies:
        copy.wait()


def cut(flags, which, qkv, last):
    span, width = last.shape
    hbm = pl.BlockSpec(memory_space=pltpu.HBM)
    return pl.pallas_call(
        functools.partial(cut_kernel, which),
        in_specs=[pl.BlockSpec(memory_space=pltpu.SMEM), hbm, hbm],
        out_specs=[pl.BlockSpec(memory_space=pltpu.VMEM)] * 4,
        out_shape=[jax.ShapeDtypeStruct((span // 2, width), jnp.bfloat16)] * 4,
        scratch_shapes=[pltpu.SemaphoreType.DMA((4,))],
        compiler_params=pltpu.CompilerParams(vmem_limit_bytes=60 * 2**20),
        name="cut",
    )(flags, qkv, last)


def assemble_kernel(layouts, group, flag_ref, *refs):
    total = sum(sum(counts) for counts, _ in layouts)
    sources, outs, sems = refs[:total], refs[total:-1], refs[-1]
    parity = flag_ref[2]
    copies = []
    at = 0
    for out, (counts, piece_total) in zip(outs, layouts):
        span = out.shape[1] // len(counts)
        for slot, count in enumerate(counts):
            for part in range(count):
                source, sem = sources[at], sems.at[at]
                at += 1
                if count == 1:
                    target = out.at[:, pl.ds(slot * span, span)]
                else:
                    half = span // 2
                    place = parity if part < piece_total else 1 - parity
                    rows = pl.ds(pl.multiple_of(slot * span + place * half, 16), half)
                    target = out.at[part % piece_total, rows]
                copies.append(pltpu.make_async_copy(source, target, sem))

    @pl.when(flag_ref[0] == group if group is not None else flag_ref[0] >= 0)
    def _():
        for copy in copies:
            copy.start()
        for copy in copies:
            copy.wait()


def assemble(flags, group, arrays):
    layouts, sources, shapes = [], [], []
    for slots in arrays:
        piece_total, span, width = slots[0][0].shape
        layouts.append((tuple(len(slot) for slot in slots), piece_total))
        sources += [piece for slot in slots for piece in slot]
        shapes.append(jax.ShapeDtypeStruct((piece_total, span * len(slots), width), jnp.bfloat16))
    hbm = pl.BlockSpec(memory_space=pltpu.HBM)
    return pl.pallas_call(
        functools.partial(assemble_kernel, tuple(layouts), group),
        in_specs=[pl.BlockSpec(memory_space=pltpu.SMEM)] + [hbm] * len(sources),
        out_specs=[pl.BlockSpec(memory_space=pltpu.VMEM)] * len(shapes),
        out_shape=shapes,
        scratch_shapes=[pltpu.SemaphoreType.DMA((len(sources),))],
        compiler_params=pltpu.CompilerParams(vmem_limit_bytes=16 * 2**20),
    )(flags, *sources)


def stage_kernel(cols, head_width, token_total, tiles, count, mode, level, group, partial, *refs):
    noised = level > 0
    flag_ref, steps_ref = refs[:2]
    refs = refs[2:]
    x_refs, refs = refs[:count], refs[count:]
    noise_refs, refs = (refs[:tiles], refs[tiles:]) if noised else (None, refs)
    temb_ref, conv_ref, gain_ref, bias_ref, prompt_ref, weight_ref, last_ref = refs[:7]
    out_refs, refs = refs[7:-6], refs[-6:]
    proj, mixed_ref, normed_ref, heads_ref, x_ref, noise_ref = refs
    positions, width = mixed_ref.shape
    rows_total = weight_ref.shape[1]
    block = positions // tiles
    chunk_total = width // LANES

    @pl.when(flag_ref[0] == group)
    def _():
        tile = flag_ref[1]
        for k in range(tiles):
            rows = pl.ds(pl.multiple_of((tile ^ k) * block, 16), block)
            if mode in (0, 1):
                x_ref[rows] = x_refs[k][mode]
            if noised:
                noise_ref[rows] = noise_refs[k][0]
        sources = [x_ref] if mode in (0, 1) else x_refs

        if noised:
            alpha_bar = alpha_bar_at(steps_ref[level])
            keep, renew = jnp.sqrt(alpha_bar), jnp.sqrt(1.0 - alpha_bar)
        place = lax.broadcasted_iota(jnp.int32, (positions, LANES), 0) % cols
        first = place == 0
        last = place == cols - 1
        gap = jnp.zeros((cols, LANES), jnp.float32)

        def mix_chunk(index, total):
            lanes = pl.ds(pl.multiple_of(index * LANES, LANES), LANES)
            value = sources[0][:, lanes].astype(jnp.float32)
            for other in sources[1:]:
                value = (value + other[:, lanes].astype(jnp.float32)).astype(jnp.bfloat16)
                value = value.astype(jnp.float32)
            if noised:
                value = keep * value + renew * noise_ref[:, lanes].astype(jnp.float32)
                value = value.astype(jnp.bfloat16).astype(jnp.float32)
            value = (value + temb_ref[:, lanes]).astype(jnp.bfloat16).astype(jnp.float32)
            before = jnp.where(first, 0.0, pltpu.roll(value, 1, 0))
            after = jnp.where(last, 0.0, pltpu.roll(value, positions - 1, 0))
            taps = conv_ref[:, lanes]

            def row_of(a):
                return (
                    taps[3 * a : 3 * a + 1] * before
                    + taps[3 * a + 1 : 3 * a + 2] * value
                    + taps[3 * a + 2 : 3 * a + 3] * after
                )

            mixed = value + row_of(1)
            mixed = mixed + jnp.concatenate([gap, row_of(0)[: positions - cols]], axis=0)
            mixed = mixed + jnp.concatenate([row_of(2)[cols:], gap], axis=0)
            mixed_ref[:, lanes] = mixed
            return total + mixed

        total = lax.fori_loop(
            0, chunk_total, mix_chunk, jnp.zeros((positions, LANES), jnp.float32)
        )
        centre = jnp.sum(total, axis=1, keepdims=True) / width

        def spread_chunk(index, total):
            lanes = pl.ds(pl.multiple_of(index * LANES, LANES), LANES)
            return total + jnp.square(mixed_ref[:, lanes] - centre)

        total = lax.fori_loop(
            0, chunk_total, spread_chunk, jnp.zeros((positions, LANES), jnp.float32), unroll=2
        )
        scale = lax.rsqrt(jnp.sum(total, axis=1, keepdims=True) / width + 1e-05)

        def norm_chunk(index, carry):
            lanes = pl.ds(pl.multiple_of(index * LANES, LANES), LANES)
            value = (mixed_ref[:, lanes] - centre) * scale
            normed_ref[:, lanes] = (value * gain_ref[:, lanes] + bias_ref[:, lanes]).astype(
                jnp.bfloat16
            )
            return carry

        lax.fori_loop(0, chunk_total, norm_chunk, 0, unroll=2)

        big = rows_total // 2
        for piece in range(3):
            for start in range(0, rows_total, big):
                rows = pl.ds(start, big)
                proj[piece, rows] = lax.dot_general(
                    weight_ref[piece, rows],
                    normed_ref[...],
                    (((1,), (1,)), ((), ())),
                    preferred_element_type=jnp.float32,
                ).astype(jnp.bfloat16)

        prompt_slots = prompt_ref.shape[2]
        pair = 2 * head_width
        usable = lax.broadcasted_iota(jnp.int32, (2 * positions, prompt_slots), 1) < token_total
        upper = lax.broadcasted_iota(jnp.int32, (positions, pair), 1) < head_width
        factor = 1.0 / math.sqrt(head_width)

        def pair_step(index, carry):
            rows = pl.ds(pl.multiple_of(index * pair, pair), pair)
            both = proj[0, rows].T
            nothing = jnp.zeros_like(both)
            queries = jnp.concatenate(
                [jnp.where(upper, both, nothing), jnp.where(upper, nothing, both)], axis=0
            )
            keys = jnp.concatenate([proj[1, rows], prompt_ref[0, rows]], axis=1)
            values = jnp.concatenate([proj[2, rows], prompt_ref[1, rows]], axis=1)
            scores = jnp.dot(queries, keys, preferred_element_type=jnp.float32)
            powers = jnp.exp(scores * factor)
            front = powers[:, :positions]
            rear = jnp.where(usable, powers[:, positions:], 0.0)
            if front.shape == rear.shape:
                whole = jnp.sum(front + rear, axis=1, keepdims=True)
            else:
                whole = jnp.sum(front, axis=1, keepdims=True) + jnp.sum(rear, axis=1, keepdims=True)
            inverse = 1.0 / whole
            soft = jnp.concatenate([front * inverse, rear * inverse], axis=1).astype(jnp.bfloat16)
            joined = lax.dot_general(
                soft, values, (((1,), (1,)), ((), ())), preferred_element_type=jnp.float32
            )
            heads_ref[:, rows] = jnp.where(upper, joined[:positions], joined[positions:]).astype(
                jnp.bfloat16
            )
            return carry

        lax.fori_loop(0, rows_total // pair, pair_step, 0, unroll=5)

        piece = 2 * LANES
        for start in range(0, width, piece):
            lanes = pl.ds(start, piece)
            update = jnp.dot(
                heads_ref[...], last_ref[0, :, lanes], preferred_element_type=jnp.float32
            )
            final = update if partial else mixed_ref[:, lanes] + update
            out_refs[0][:, lanes] = final.astype(jnp.bfloat16)


def run_stage(flags, timesteps, x, noise, vectors, prompts, weights, last, cols, head_width, tokens, tiles, mode, level, group, partial):
    noised = noise is not None
    width = weights.shape[2]
    positions = x[0].shape[0] if mode == 2 else x[0].shape[1] * tiles
    rows = weights.shape[1]
    vmem = pl.BlockSpec(memory_space=pltpu.VMEM)
    smem = pl.BlockSpec(memory_space=pltpu.SMEM)
    inputs = list(x) + (noise if noised else []) + list(vectors) + [prompts, weights, last]
    spare = (positions, width)
    return pl.pallas_call(
        functools.partial(
            stage_kernel, cols, head_width, tokens, tiles, len(x), mode, level if noised else 0,
            group, partial,
        ),
        in_specs=[smem, smem] + [vmem] * len(inputs),
        out_specs=[vmem],
        out_shape=[jax.ShapeDtypeStruct((positions, width), jnp.bfloat16)],
        scratch_shapes=[
            pltpu.VMEM((3, rows, positions), jnp.bfloat16),
            pltpu.VMEM((positions, width), jnp.float32),
            pltpu.VMEM((positions, width), jnp.bfloat16),
            pltpu.VMEM((positions, rows), jnp.bfloat16),
            pltpu.VMEM(spare if mode != 2 else (16, LANES), jnp.bfloat16),
            pltpu.VMEM(spare if noised else (16, LANES), jnp.bfloat16),
        ],
        compiler_params=pltpu.CompilerParams(vmem_limit_bytes=24 * 2**20),
    )(flags, timesteps, *inputs)[0]


def per_device(
    latents,
    prompt_tokens,
    fresh_noise,
    timesteps,
    entry_order,
    timestep_weight,
    conv_kernel,
    norm_gain,
    layer_norm_bias,
    qkv_weight,
    prompt_weight,
    out_weight,
):
    sections = lax.axis_size("section")
    tiles = lax.axis_size("tile")
    parts = lax.axis_size("batch")
    section = lax.axis_index("section")
    tile = lax.axis_index("tile")
    micro, rows_here, cols, width = latents.shape
    steps = timesteps.shape[0]
    head_width = width // HEADS
    span = qkv_weight.shape[3]
    tokens = prompt_tokens.shape[1]
    assert micro == tiles and tiles & (tiles - 1) == 0

    features = time_features(timesteps, timestep_weight.shape[1] // 2)
    temb = jnp.dot(features, timestep_weight[0], preferred_element_type=jnp.float32)

    own_qkv = qkv_weight[0].transpose(1, 2, 0)
    own_out = out_weight[0]
    paired = parts % 2 == 0
    parity = lax.axis_index("batch") % 2 if paired else jnp.int32(0)
    flags = jnp.stack([section, tile, parity]).astype(jnp.int32)

    def exchanged(source, axis, mask):
        moved = []
        for piece in source:
            moved.append(swapped(piece, axis, mask))
        return moved

    halves = list(cut(flags, 0, own_qkv, own_out))
    halves, own_qkv, own_out, prompt_tokens, latents, fresh_noise = lax.optimization_barrier(
        (halves, own_qkv, own_out, prompt_tokens, latents, fresh_noise)
    )

    def picked(stack):
        return [lax.dynamic_index_in_dim(stack, tile ^ k, 0, False) for k in range(tiles)]

    def sent(mine, group=None):
        first = 0 if group is None else group * tiles
        pairs = [[(first + t, first + (t ^ k)) for t in range(tiles)] for k in range(tiles)]
        axis = "tile" if group is None else ("section", "tile")
        result = list(mine[:1])
        for k in range(1, tiles):
            result.append(lax.ppermute(mine[k], axis, pairs[k]))
        return result

    def across(stack, group=None):
        return sent(picked(stack), group)

    def in_order(entries):
        stacked = jnp.stack(entries)
        return jnp.stack(
            [lax.dynamic_index_in_dim(stacked, tile ^ r, 0, False) for r in range(tiles)]
        )

    padded = -(-tokens // LANES) * LANES
    prompt_rows = prompt_weight[0].transpose(1, 2, 0).reshape(2 * span, -1)

    def relayed(near, bit):
        if not paired:
            return exchanged(list(cut(flags, 1, own_qkv, own_out)), "tile", bit)
        far = []
        for piece in range(4):
            far.append(swapped(near[piece], "batch", 1))
        return far

    paired_start = tiles == 4 and sections > 1
    far_mask = tiles // 2
    slots = [None] * tiles
    near = {bit: exchanged(halves, "tile", bit) for bit in [1 << i for i in range(1, tiles.bit_length() - 1)]}
    token_rows = jnp.pad(prompt_tokens, ((0, 0), (0, padded - tokens), (0, 0)))
    prompt_local = project_prompts(token_rows, prompt_rows).reshape(micro, 2, span, padded)

    def two(stack, k):
        return jnp.stack(
            [lax.dynamic_index_in_dim(stack, tile ^ k ^ j, 0, False) for j in (0, far_mask)]
        )

    latent_rows = latents.reshape(micro * rows_here * cols, width)
    picks = picked(prompt_local)
    if paired_start:
        picks[:2] = [two(prompt_local, 0), two(prompt_local, 1)]
    moved = sent(picks, None)
    if paired_start:
        pair_prompts = [[piece[j] for piece in moved[:2]] for j in range(2)]
        prompts = [[piece[0]] for piece in moved[:2]] + [[piece] for piece in moved[2:]]
        masks = tuple((k, k ^ far_mask) for k in range(tiles))
        x = sent(pick(flags, None, latent_rows, rows_here * cols, masks, 60), 0)
    else:
        prompts = [[piece] for piece in moved]
        masks = tuple((k,) for k in range(tiles))
        x = sent(pick(flags, None, latent_rows, rows_here * cols, masks, 60), 0)
    slots[0] = [own_qkv, own_out[None]]
    if tiles > 1:
        slots[1] = exchanged(slots[0], "tile", 1)
    for bit in near:
        slots[bit] = near[bit] + relayed(near[bit], bit)
    for slot in range(3, tiles):
        bit = 1 << (slot.bit_length() - 1)
        if slot != bit:
            slots[slot] = [
                None if index % 4 == 3 else swapped(piece, "tile", slot - bit)
                for index, piece in enumerate(slots[bit])
            ]

    noises = [None]
    for level in range(1, steps):
        rows = fresh_noise[level - 1].reshape(micro * rows_here * cols, width)
        noises.append(
            pick(flags, entry_order, rows, rows_here * cols, tuple((k,) for k in range(tiles)), 16)
        )
    tembs = [temb[level : level + 1] for level in range(steps)]
    taps = conv_kernel[0]
    if paired_start:
        chip_weights, chip_last, *chip_prompts = assemble(
            flags,
            0,
            [[slots[0][:1], slots[1][:1]], [slots[0][1:], slots[1][1:]]]
            + [[[p] for p in pair] for pair in pair_prompts],
        )
        begun = []
        for j in (1, 0):
            begun.append(
                run_stage(
                    flags, timesteps, x, None,
                    [tembs[0], taps, norm_gain, layer_norm_bias],
                    chip_prompts[j], chip_weights, chip_last, cols, head_width, tokens, tiles,
                    j, 0, 0, j == 1,
                )
            )
        partner, mine = begun
        pairs = [(t, tiles + t) for t in range(tiles)]
        crossed = [(t, tiles + (t ^ far_mask)) for t in range(tiles)]
        x = [lax.ppermute(mine, ("section", "tile"), pairs)]
        x.append(lax.ppermute(partner, ("section", "tile"), crossed))

    firsts = [slot[:1] if len(slot) == 2 else slot[:3] + slot[4:7] for slot in slots]
    firsts, prompts, tembs, taps = lax.optimization_barrier((firsts, prompts, tembs, taps))
    weights = assemble(flags, None, [firsts])[0]
    for bit in near:
        slots[bit][7], weights = lax.optimization_barrier((slots[bit][7], weights))
    lasts = [None] * tiles
    for slot in range(tiles):
        bit = 1 << (slot.bit_length() - 1) if slot else 0
        if slot < 2:
            lasts[slot] = slots[slot][1:]
        elif slot == bit:
            lasts[slot] = [slots[slot][3], slots[slot][7]]
        else:
            lasts[slot] = exchanged([slots[bit][3], slots[bit][7]], "tile", slot - bit)
    last, prompts = assemble(flags, None, [lasts, prompts])
    noises = [None] + [sent(mine, 0) for mine in noises[1:]]

    stages = steps * sections
    for stage in range(1 if paired_start else 0, stages):
        level, group = divmod(stage, sections)
        noise = noises[level] if group == 0 else None
        x = run_stage(
            flags, timesteps, x, noise,
            [tembs[level], taps, norm_gain, layer_norm_bias],
            prompts, weights, last, cols, head_width, tokens, tiles, 0 if stage == 0 else 2,
            level, group, False,
        )
        if stage + 1 < stages:
            x = [lax.ppermute(x, "section", [(group, (group + 1) % sections)])]

    share = width // sections
    final = sections - 1
    mine = x[:, final * share :]
    for other in range(final):
        piece = x[:, other * share : (other + 1) * share]
        mine = jnp.where(section == other, lax.ppermute(piece, "section", [(final, other)]), mine)
    blocks = mine.reshape(tiles, rows_here, cols, share)
    return in_order(across(blocks))


def solution(mesh):
    placed = (
        P("batch", "tile", None, None),
        P("batch", None, None),
        P(None, "batch", "tile", None, None),
        P(),
        P("batch"),
        P("section", None, None),
        P("section", None, None),
        P("section", None),
        P("section", None),
        P("section", None, None, "tile"),
        P("section", None, None, "tile"),
        P("section", "tile", None),
    )

    return jax.shard_map(
        per_device,
        mesh=mesh,
        in_specs=placed,
        out_specs=P("batch", "tile", None, "section"),
        check_vma=False,
    )
```

profile of v0, /device:TPU:0, one launch (start us, length us, event | category | flops | bytes accessed | tf_op | source)
XLA Modules:
  0.0 232.4 jit_solution(8787915427191886770)
XLA Ops:
  0.6 3.4 %cut.1 = (bf16[160,1280]{1,0:T(8,128)(2,1)}, bf16[160,1280]{1,0:T(8,128)(2,1)}, bf16[160,1280]{1,0:T(8,128)(2,1)}, bf16[160,1280]{1,0:T(8,128)(2,1)}) custom-call(s32[3]{0:T(128)} %pad_add_fusion.flag_ref.refs_0_, bf16[3,320,1280]{2,1,0:T(8,128)(2,1)} %bitcast.44, bf16[320,1280]{1,0:T(8,128)(2,1)} %bitcast.57), custom_call_target="tpu_custom_call" | custom-call | tf_op jit(solution)/shard_map/cut/pallas_call | solution.py:124
  4.6 2.0 copy.13
  6.6 1.6 pad.4.token_ref
  8.2 4.6 %prompts.1 = bf16[4,640,128]{2,1,0:T(8,128)(2,1)} custom-call(bf16[4,128,2048]{2,1,0:T(8,128)(2,1)} %pad.4.token_ref, bf16[640,2048]{1,0:T(8,128)(2,1)} %bitcast.60), custom_call_target="tpu_custom_call" | custom-call | tf_op jit(solution)/shard_map/prompts/pallas_call | solution.py:54
  12.8 2.0 dynamic-slice_bitcast_fusion
  14.7 2.5 %collective-permute-start.20 = (bf16[2,320,128]{2,1,0:T(8,128)(2,1)S(1)}, bf16[2,320,128]{2,1,0:T(8,128)(2,1)S(1)}, u32[]{:S(2)}, u32[]{:S(2)}) collective-permute-start(bf16[2,320,128]{2,1,0:T(8,128)(2,1)S(1)} %get-tuple-element.106.refs_6_), channel_id=1, source_target_pairs={{0,2},{1,3},{2,0},{3,1},{4,6},{5,7},{6,4},{7,5},{8,10},{9,11},{10,... | collective-permute-start | bytes 491528 | tf_op jit(solution)/shard_map/ppermute | solution.py:406
  17.6 1.9 collective-permute-start.8
  19.5 2.8 %collective-permute-done.20.refs_8_ = bf16[2,320,128]{2,1,0:T(8,128)(2,1)S(1)} collective-permute-done((bf16[2,320,128]{2,1,0:T(8,128)(2,1)S(1)}, bf16[2,320,128]{2,1,0:T(8,128)(2,1)S(1)}, u32[]{:S(2)}, u32[]{:S(2)}) %collective-permute-start.20) | collective-permute-done | bytes 163872 | tf_op jit(solution)/shard_map/ppermute | solution.py:406
  23.0 2.0 collective-permute-start.9
  26.0 1.5 collective-permute-start.10
  28.2 6.4 %collective-permute-done.8.refs_2_ = bf16[160,1280]{1,0:T(8,128)(2,1)S(1)} collective-permute-done((bf16[160,1280]{1,0:T(8,128)(2,1)}, bf16[160,1280]{1,0:T(8,128)(2,1)S(1)}, u32[]{:S(2)}, u32[]{:S(2)}) %collective-permute-start.8) | collective-permute-done | bytes 409632 | tf_op jit(solution)/shard_map/ppermute | solution.py:36
  34.6 2.0 collective-permute-start.11
  36.6 6.8 %collective-permute-done.9.refs_3_ = bf16[160,1280]{1,0:T(8,128)(2,1)S(1)} collective-permute-done((bf16[160,1280]{1,0:T(8,128)(2,1)}, bf16[160,1280]{1,0:T(8,128)(2,1)S(1)}, u32[]{:S(2)}, u32[]{:S(2)}) %collective-permute-start.9) | collective-permute-done | bytes 409632 | tf_op jit(solution)/shard_map/ppermute | solution.py:36
  43.4 2.0 collective-permute-start.12
  45.4 6.8 %collective-permute-done.10.refs_4_ = bf16[160,1280]{1,0:T(8,128)(2,1)S(1)} collective-permute-done((bf16[160,1280]{1,0:T(8,128)(2,1)}, bf16[160,1280]{1,0:T(8,128)(2,1)S(1)}, u32[]{:S(2)}, u32[]{:S(2)}) %collective-permute-start.10) | collective-permute-done | bytes 409632 | tf_op jit(solution)/shard_map/ppermute | solution.py:36
  52.2 2.0 collective-permute-start.13
  54.1 6.7 %collective-permute-done.22.refs_2_ = bf16[160,1280]{1,0:T(8,128)(2,1)} collective-permute-done((bf16[160,1280]{1,0:T(8,128)(2,1)}, bf16[160,1280]{1,0:T(8,128)(2,1)}, u32[]{:S(2)}, u32[]{:S(2)}) %collective-permute-start.22) | collective-permute-done | bytes 409632 | tf_op jit(solution)/shard_map/ppermute | solution.py:36
  60.8 0.7 copy-done.9
  62.2 0.8 copy-done.11
  62.9 0.7 copy-done.13
  64.2 0.7 copy-done.15
  65.4 0.8 copy-done.19
  66.3 1.7 collective-permute-start.23
  68.0 0.8 copy-done.21
  69.0 0.8 copy-done.23
  70.1 2.7 %shard_map.118 = (bf16[2,32,1280]{2,1,0:T(8,128)(2,1)}, bf16[2,32,1280]{2,1,0:T(8,128)(2,1)}, bf16[2,32,1280]{2,1,0:T(8,128)(2,1)}, bf16[2,32,1280]{2,1,0:T(8,128)(2,1)}) custom-call(s32[3]{0:T(128)} %pad_add_fusion.flag_ref.refs_0_, bf16[128,1280]{1,0:T(8,128)(2,1)} %bitcast.63), custom_call_target="tpu_custom_call" | custom-call | tf_op jit(solution)/shard_map/pallas_call | solution.py:96
  72.8 0.8 copy.17
  73.6 2.1 collective-permute-start
  75.8 3.4 %collective-permute-start.1 = (bf16[2,32,1280]{2,1,0:T(8,128)(2,1)}, bf16[2,32,1280]{2,1,0:T(8,128)(2,1)S(1)}, u32[]{:S(2)}, u32[]{:S(2)}) collective-permute-start(bf16[2,32,1280]{2,1,0:T(8,128)(2,1)} %get-tuple-element.62), channel_id=1, source_target_pairs={{0,2},{1,3},{2,0},{3,1},{4,6},{5,7},{6,4},{7,5}} | collective-permute-start | bytes 491528 | tf_op jit(solution)/shard_map/ppermute | solution.py:406
  79.2 2.0 collective-permute-start.2
  81.3 1.0 slice_bitcast_fusion
  82.3 1.0 copy-done.10
  83.3 1.0 copy-done.12
  84.3 1.0 copy-done.14
  85.3 1.0 copy-done.16
  86.3 1.0 copy-done.18
  87.3 1.0 copy-done.20
  88.3 1.0 copy-done.22
  89.3 1.0 copy-done.24
  90.3 3.8 %shard_map.122.refs_9_.refs_8_.refs_12_ = bf16[3,1280,1280]{2,1,0:T(8,128)(2,1)S(1)} custom-call(s32[3]{0:T(128)S(1)} %copy-done.30, bf16[3,320,1280]{2,1,0:T(8,128)(2,1)S(1)} %bitcast.46, bf16[3,320,1280]{2,1,0:T(8,128)(2,1)} %collective-permute-done.3.refs_1_, bf16[160,1280]{1,0:T(8,128)(2,1)S(1)} %copy-done.10, bf16[160,1280]{1,0:T(8,128)(2,1)S(1)} %copy-done.12, ...), custom_call_target="tpu_custom_call" | custom-call | tf_op jit(solution)/shard_map/pallas_call | solution.py:172
  94.8 2.5 %shard_map.119 = (bf16[3,640,1280]{2,1,0:T(8,128)(2,1)S(1)}, bf16[1,640,1280]{2,1,0:T(8,128)(2,1)S(1)}, bf16[2,640,128]{2,1,0:T(8,128)(2,1)S(1)}, bf16[2,640,128]{2,1,0:T(8,128)(2,1)S(1)}) custom-call(s32[3]{0:T(128)S(1)} %copy-done.30, bf16[3,320,1280]{2,1,0:T(8,128)(2,1)S(1)} %bitcast.47, bf16[3,320,1280]{2,1,0:T(8,128)(2,1)} %collective-permute-done.3.refs_1_, ...), custom_call_target="tpu_custom_call" | custom-call | tf_op jit(solution)/shard_map/pallas_call | solution.py:172
  97.4 4.1 %shard_map.120 = bf16[128,1280]{1,0:T(8,128)(2,1)S(1)} custom-call(s32[3]{0:T(128)S(1)} %copy-done.30, s32[2]{0:T(128)S(1)} %copy-done.31, bf16[2,32,1280]{2,1,0:T(8,128)(2,1)S(1)} %copy-done.6, bf16[2,32,1280]{2,1,0:T(8,128)(2,1)S(1)} %collective-permute-done.refs_3_, bf16[2,32,1280]{2,1,0:T(8,128)(2,1)S(1)} %collective-permute-done.1.refs_4_, ...), custom_call_target="tpu_custom_call" | custom-call | tf_op jit(solution)/shard_map/pallas_call | solution.py:331
  101.5 1.3 collective-permute-start.6
  102.8 4.1 %shard_map.121 = bf16[128,1280]{1,0:T(8,128)(2,1)S(1)} custom-call(s32[3]{0:T(128)S(1)} %copy-done.30, s32[2]{0:T(128)S(1)} %copy-done.31, bf16[2,32,1280]{2,1,0:T(8,128)(2,1)S(1)} %copy-done.6, bf16[2,32,1280]{2,1,0:T(8,128)(2,1)S(1)} %collective-permute-done.refs_3_, bf16[2,32,1280]{2,1,0:T(8,128)(2,1)S(1)} %collective-permute-done.1.refs_4_, ...), custom_call_target="tpu_custom_call" | custom-call | tf_op jit(solution)/shard_map/pallas_call | solution.py:331
  106.9 1.3 collective-permute-start.7
  108.3 2.0 shard_map.123
  110.9 6.8 %collective-permute-done.7.refs_3_ = bf16[128,1280]{1,0:T(8,128)(2,1)S(1)} collective-permute-done((bf16[128,1280]{1,0:T(8,128)(2,1)S(1)}, bf16[128,1280]{1,0:T(8,128)(2,1)S(1)}, u32[]{:S(2)}, u32[]{:S(2)}) %collective-permute-start.7) | collective-permute-done | bytes 327712 | tf_op jit(solution)/shard_map/ppermute | solution.py:497
  119.7 0.8 collective-permute-start.27
  121.1 1.3 collective-permute-start.28
  122.4 1.0 shard_map.127
  123.4 1.9 collective-permute-start.29
  125.3 3.4 %collective-permute-start.30 = (bf16[1,32,1280]{2,1,0:T(8,128)(2,1)S(1)}, bf16[1,32,1280]{2,1,0:T(8,128)(2,1)S(1)}, u32[]{:S(2)}, u32[]{:S(2)}) collective-permute-start(bf16[1,32,1280]{2,1,0:T(8,128)(2,1)S(1)} %get-tuple-element.102), channel_id=1, source_target_pairs={{0,2},{1,3},{2,0},{3,1},{4,6},{5,7},{6,4},{7,5}} | collective-permute-start | bytes 245768 | tf_op jit(solution)/shard_map/ppermute | solution.py:406
  128.8 2.2 collective-permute-start.31
  131.0 1.0 collective-permute-done.30.refs_5_
  132.1 2.9 %collective-permute-done.31.refs_6_ = bf16[1,32,1280]{2,1,0:T(8,128)(2,1)S(1)} collective-permute-done((bf16[1,32,1280]{2,1,0:T(8,128)(2,1)S(1)}, bf16[1,32,1280]{2,1,0:T(8,128)(2,1)S(1)}, u32[]{:S(2)}, u32[]{:S(2)}) %collective-permute-start.31) | collective-permute-done | bytes 81952 | tf_op jit(solution)/shard_map/ppermute | solution.py:406
  135.0 34.2 %collective-permute-done.28.refs_2_ = bf16[128,1280]{1,0:T(8,128)(2,1)S(1)} collective-permute-done((bf16[128,1280]{1,0:T(8,128)(2,1)S(1)}, bf16[128,1280]{1,0:T(8,128)(2,1)S(1)}, u32[]{:S(2)}, u32[]{:S(2)}) %collective-permute-start.28) | collective-permute-done | bytes 327712 | tf_op jit(solution)/shard_map/ppermute | solution.py:527
  169.2 6.7 %shard_map.128 = bf16[128,1280]{1,0:T(8,128)(2,1)S(1)} custom-call(s32[3]{0:T(128)S(1)} %copy-done.30, s32[2]{0:T(128)S(1)} %copy-done.31, bf16[128,1280]{1,0:T(8,128)(2,1)S(1)} %collective-permute-done.28.refs_2_, bf16[1,32,1280]{2,1,0:T(8,128)(2,1)S(1)} %get-tuple-element.100.refs_3_, bf16[1,32,1280]{2,1,0:T(8,128)(2,1)S(1)} %collective-permute-done.29.refs_4_, ...), custom_call_target="tpu_custom_call" | custom-call | tf_op jit(solution)/shard_map/pallas_call | solution.py:331
  176.0 1.3 collective-permute-start.32
  177.3 5.5 %collective-permute-done.32.refs_2_ = bf16[128,1280]{1,0:T(8,128)(2,1)S(1)} collective-permute-done((bf16[128,1280]{1,0:T(8,128)(2,1)S(1)}, bf16[128,1280]{1,0:T(8,128)(2,1)S(1)}, u32[]{:S(2)}, u32[]{:S(2)}) %collective-permute-start.32) | collective-permute-done | bytes 327712 | tf_op jit(solution)/shard_map/ppermute | solution.py:527
  184.0 0.8 shard_map.130
  187.5 1.3 collective-permute-start.37
  188.9 38.7 %collective-permute-done.37 = bf16[128,320]{1,0:T(8,128)(2,1)S(1)} collective-permute-done((bf16[128,320]{1,0:T(8,128)(2,1)S(1)}, bf16[128,320]{1,0:T(8,128)(2,1)S(1)}, u32[]{:S(2)}, u32[]{:S(2)}) %collective-permute-start.37) | collective-permute-done | bytes 81952 | tf_op jit(solution)/shard_map/ppermute | solution.py:534
  228.3 1.3 collective-permute-start.38
  229.6 1.4 collective-permute-done.40
  (121 shorter events, 15.9 us)
Async XLA Ops:
  0.0 65.2 %copy-start = (bf16[1,320,1280]{2,1,0:T(8,128)(2,1)S(1)}, bf16[1,320,1280]{2,1,0:T(8,128)(2,1)}, u32[]{:S(2)}) copy-start(bf16[1,320,1280]{2,1,0:T(8,128)(2,1)} %param.17) | copy-start | bytes 2457604
  0.0 4.0 %copy-start.1 = (bf16[1,1280,3,320]{1,3,2,0:T(8,128)(2,1)S(1)}, bf16[1,1280,3,320]{1,3,2,0:T(8,128)(2,1)}, u32[]{:S(2)}) copy-start(bf16[1,1280,3,320]{1,3,2,0:T(8,128)(2,1)} %param.21) | copy-start | bytes 7372804
  4.0 75.2 %collective-permute-start.3 = (bf16[3,320,1280]{2,1,0:T(8,128)(2,1)S(1)}, bf16[3,320,1280]{2,1,0:T(8,128)(2,1)}, u32[]{:S(2)}, u32[]{:S(2)}) collective-permute-start(bf16[3,320,1280]{2,1,0:T(8,128)(2,1)S(1)} %bitcast.45), channel_id=1, source_target_pairs={{0,1},{1,0},{2,3},{3,2},{4,5},{5,4},{6,7},{7,6},{8,9},{9,8},{10,11... | collective-permute-start | bytes 7372808 | tf_op jit(solution)/shard_map/ppermute | solution.py:36
  8.2 53.4 %copy-start.31 = (s32[2]{0:T(128)S(1)}, s32[2]{0:T(128)}, u32[]{:S(2)}) copy-start(s32[2]{0:T(128)} %refs_1_.17) | copy-start | bytes 28
  12.8 69.5 %copy-start.30 = (s32[3]{0:T(128)S(1)}, s32[3]{0:T(128)}, u32[]{:S(2)}) copy-start(s32[3]{0:T(128)} %pad_add_fusion.flag_ref.refs_0_) | copy-start | bytes 40
  14.7 50.4 %copy-start.4 = (bf16[2,320,128]{2,1,0:T(8,128)(2,1)}, bf16[2,320,128]{2,1,0:T(8,128)(2,1)S(1)}, u32[]{:S(2)}) copy-start(bf16[2,320,128]{2,1,0:T(8,128)(2,1)S(1)} %get-tuple-element.106.refs_6_) | copy-start | bytes 491524
  14.7 7.6 %collective-permute-start.20 = (bf16[2,320,128]{2,1,0:T(8,128)(2,1)S(1)}, bf16[2,320,128]{2,1,0:T(8,128)(2,1)S(1)}, u32[]{:S(2)}, u32[]{:S(2)}) collective-permute-start(bf16[2,320,128]{2,1,0:T(8,128)(2,1)S(1)} %get-tuple-element.106.refs_6_), channel_id=1, source_target_pairs={{0,2},{1,3},{2,0},{3,1},{4,6},{5,7},{6,4},{7,5},{8,10},{9,11},{10,... | collective-permute-start | bytes 491528 | tf_op jit(solution)/shard_map/ppermute | solution.py:406
  17.3 8.1 %collective-permute-start.21 = (bf16[2,320,128]{2,1,0:T(8,128)(2,1)S(1)}, bf16[2,320,128]{2,1,0:T(8,128)(2,1)S(1)}, u32[]{:S(2)}, u32[]{:S(2)}) collective-permute-start(bf16[2,320,128]{2,1,0:T(8,128)(2,1)S(1)} %get-tuple-element.105), channel_id=1, source_target_pairs={{0,3},{1,2},{2,1},{3,0},{4,7},{5,6},{6,5},{7,4},{8,11},{9,10},{10,... | collective-permute-start | bytes 491528 | tf_op jit(solution)/shard_map/ppermute | solution.py:406
  17.4 10.1 %collective-permute-start.5 = (bf16[2,2,320,128]{3,2,1,0:T(8,128)(2,1)S(1)}, bf16[2,2,320,128]{3,2,1,0:T(8,128)(2,1)S(1)}, u32[]{:S(2)}, u32[]{:S(2)}) collective-permute-start(bf16[2,2,320,128]{3,2,1,0:T(8,128)(2,1)S(1)} %pad_maximum_fusion), channel_id=1, source_target_pairs={{0,1},{1,0},{2,3},{3,2},{4,5},{5,4},{6,7},{7,6},{8,9},{9,8},{10,11... | collective-permute-start | bytes 983048 | tf_op jit(solution)/shard_map/ppermute | solution.py:406
  17.6 17.0 %collective-permute-start.8 = (bf16[160,1280]{1,0:T(8,128)(2,1)}, bf16[160,1280]{1,0:T(8,128)(2,1)S(1)}, u32[]{:S(2)}, u32[]{:S(2)}) collective-permute-start(bf16[160,1280]{1,0:T(8,128)(2,1)} %get-tuple-element.71), channel_id=1, source_target_pairs={{0,2},{1,3},{2,0},{3,1},{4,6},{5,7},{6,4},{7,5},{8,10},{9,11},{10,... | collective-permute-start | bytes 1228808 | tf_op jit(solution)/shard_map/ppermute | solution.py:36
  23.0 20.4 %collective-permute-start.9 = (bf16[160,1280]{1,0:T(8,128)(2,1)}, bf16[160,1280]{1,0:T(8,128)(2,1)S(1)}, u32[]{:S(2)}, u32[]{:S(2)}) collective-permute-start(bf16[160,1280]{1,0:T(8,128)(2,1)} %get-tuple-element.72), channel_id=1, source_target_pairs={{0,2},{1,3},{2,0},{3,1},{4,6},{5,7},{6,4},{7,5},{8,10},{9,11},{10,... | collective-permute-start | bytes 1228808 | tf_op jit(solution)/shard_map/ppermute | solution.py:36
  26.0 26.1 %collective-permute-start.10 = (bf16[160,1280]{1,0:T(8,128)(2,1)}, bf16[160,1280]{1,0:T(8,128)(2,1)S(1)}, u32[]{:S(2)}, u32[]{:S(2)}) collective-permute-start(bf16[160,1280]{1,0:T(8,128)(2,1)} %get-tuple-element.73), channel_id=1, source_target_pairs={{0,2},{1,3},{2,0},{3,1},{4,6},{5,7},{6,4},{7,5},{8,10},{9,11},{10,... | collective-permute-start | bytes 1228808 | tf_op jit(solution)/shard_map/ppermute | solution.py:36
  27.5 33.3 %collective-permute-start.22 = (bf16[160,1280]{1,0:T(8,128)(2,1)}, bf16[160,1280]{1,0:T(8,128)(2,1)}, u32[]{:S(2)}, u32[]{:S(2)}) collective-permute-start(bf16[160,1280]{1,0:T(8,128)(2,1)} %get-tuple-element.76), channel_id=1, source_target_pairs={{0,2},{1,3},{2,0},{3,1},{4,6},{5,7},{6,4},{7,5},{8,10},{9,11},{10,... | collective-permute-start | bytes 1228808 | tf_op jit(solution)/shard_map/ppermute | solution.py:36
  34.6 27.0 %collective-permute-start.11 = (bf16[160,1280]{1,0:T(8,128)(2,1)S(1)}, bf16[160,1280]{1,0:T(8,128)(2,1)S(1)}, u32[]{:S(2)}, u32[]{:S(2)}) collective-permute-start(bf16[160,1280]{1,0:T(8,128)(2,1)S(1)} %collective-permute-done.8.refs_2_), channel_id=1, source_target_pairs={{0,4},{4,0},{1,5},{5,1},{2,6},{6,2},{3,7},{7,3},{8,12},{12,8},{9,1... | collective-permute-start | bytes 1228808 | tf_op jit(solution)/shard_map/ppermute | solution.py:36
  43.4 19.5 %collective-permute-start.12 = (bf16[160,1280]{1,0:T(8,128)(2,1)S(1)}, bf16[160,1280]{1,0:T(8,128)(2,1)}, u32[]{:S(2)}, u32[]{:S(2)}) collective-permute-start(bf16[160,1280]{1,0:T(8,128)(2,1)S(1)} %collective-permute-done.9.refs_3_), channel_id=1, source_target_pairs={{0,4},{4,0},{1,5},{5,1},{2,6},{6,2},{3,7},{7,3},{8,12},{12,8},{9,1... | collective-permute-start | bytes 1228808 | tf_op jit(solution)/shard_map/ppermute | solution.py:36
  52.2 11.5 %collective-permute-start.13 = (bf16[160,1280]{1,0:T(8,128)(2,1)S(1)}, bf16[160,1280]{1,0:T(8,128)(2,1)}, u32[]{:S(2)}, u32[]{:S(2)}) collective-permute-start(bf16[160,1280]{1,0:T(8,128)(2,1)S(1)} %collective-permute-done.10.refs_4_), channel_id=1, source_target_pairs={{0,4},{4,0},{1,5},{5,1},{2,6},{6,2},{3,7},{7,3},{8,12},{12,8},{9,1... | collective-permute-start | bytes 1228808 | tf_op jit(solution)/shard_map/ppermute | solution.py:36
  60.8 4.2 %collective-permute-start.14 = (bf16[160,1280]{1,0:T(8,128)(2,1)S(1)}, bf16[160,1280]{1,0:T(8,128)(2,1)S(1)}, u32[]{:S(2)}, u32[]{:S(2)}) collective-permute-start(bf16[160,1280]{1,0:T(8,128)(2,1)S(1)} %collective-permute-done.8.refs_2_), channel_id=1, source_target_pairs={{0,1},{1,0},{2,3},{3,2},{4,5},{5,4},{6,7},{7,6},{8,9},{9,8},{10,11... | collective-permute-start | bytes 1228808 | tf_op jit(solution)/shard_map/ppermute | solution.py:36
  61.6 3.8 %collective-permute-start.15 = (bf16[160,1280]{1,0:T(8,128)(2,1)S(1)}, bf16[160,1280]{1,0:T(8,128)(2,1)S(1)}, u32[]{:S(2)}, u32[]{:S(2)}) collective-permute-start(bf16[160,1280]{1,0:T(8,128)(2,1)S(1)} %collective-permute-done.9.refs_3_), channel_id=1, source_target_pairs={{0,1},{1,0},{2,3},{3,2},{4,5},{5,4},{6,7},{7,6},{8,9},{9,8},{10,11... | collective-permute-start | bytes 1228808 | tf_op jit(solution)/shard_map/ppermute | solution.py:36
  62.9 5.1 %collective-permute-start.16 = (bf16[160,1280]{1,0:T(8,128)(2,1)S(1)}, bf16[160,1280]{1,0:T(8,128)(2,1)S(1)}, u32[]{:S(2)}, u32[]{:S(2)}) collective-permute-start(bf16[160,1280]{1,0:T(8,128)(2,1)S(1)} %collective-permute-done.10.refs_4_), channel_id=1, source_target_pairs={{0,1},{1,0},{2,3},{3,2},{4,5},{5,4},{6,7},{7,6},{8,9},{9,8},{10,11... | collective-permute-start | bytes 1228808 | tf_op jit(solution)/shard_map/ppermute | solution.py:36
  63.7 5.3 %collective-permute-start.17 = (bf16[160,1280]{1,0:T(8,128)(2,1)S(1)}, bf16[160,1280]{1,0:T(8,128)(2,1)S(1)}, u32[]{:S(2)}, u32[]{:S(2)}) collective-permute-start(bf16[160,1280]{1,0:T(8,128)(2,1)S(1)} %collective-permute-done.11.refs_5_), channel_id=1, source_target_pairs={{0,1},{1,0},{2,3},{3,2},{4,5},{5,4},{6,7},{7,6},{8,9},{9,8},{10,11... | collective-permute-start | bytes 1228808 | tf_op jit(solution)/shard_map/ppermute | solution.py:36
  65.1 3.9 %copy-start.17 = (bf16[160,1280]{1,0:T(8,128)(2,1)}, bf16[160,1280]{1,0:T(8,128)(2,1)S(1)}, u32[]{:S(2)}) copy-start(bf16[160,1280]{1,0:T(8,128)(2,1)S(1)} %collective-permute-done.14.refs_8_) | copy-start | bytes 1228804
  65.1 29.6 %collective-permute-start.4 = (bf16[1,320,1280]{2,1,0:T(8,128)(2,1)}, bf16[1,320,1280]{2,1,0:T(8,128)(2,1)S(1)}, u32[]{:S(2)}, u32[]{:S(2)}) collective-permute-start(bf16[1,320,1280]{2,1,0:T(8,128)(2,1)} %param.23), channel_id=1, source_target_pairs={{0,1},{1,0},{2,3},{3,2},{4,5},{5,4},{6,7},{7,6},{8,9},{9,8},{10,11... | collective-permute-start | bytes 2457608 | tf_op jit(solution)/shard_map/ppermute | solution.py:36
  66.3 27.9 %collective-permute-start.23 = (bf16[160,1280]{1,0:T(8,128)(2,1)}, bf16[160,1280]{1,0:T(8,128)(2,1)}, u32[]{:S(2)}, u32[]{:S(2)}) collective-permute-start(bf16[160,1280]{1,0:T(8,128)(2,1)} %collective-permute-done.22.refs_2_), channel_id=1, source_target_pairs={{0,4},{4,0},{1,5},{5,1},{2,6},{6,2},{3,7},{7,3},{8,12},{12,8},{9,1... | collective-permute-start | bytes 1228808 | tf_op jit(solution)/shard_map/ppermute | solution.py:36
  68.8 4.9 %collective-permute-start.18 = (bf16[160,1280]{1,0:T(8,128)(2,1)}, bf16[160,1280]{1,0:T(8,128)(2,1)}, u32[]{:S(2)}, u32[]{:S(2)}) collective-permute-start(bf16[160,1280]{1,0:T(8,128)(2,1)} %collective-permute-done.12.refs_6_), channel_id=1, source_target_pairs={{0,1},{1,0},{2,3},{3,2},{4,5},{5,4},{6,7},{7,6},{8,9},{9,8},{10,11... | collective-permute-start | bytes 1228808 | tf_op jit(solution)/shard_map/ppermute | solution.py:36
  69.8 6.0 %collective-permute-start.19 = (bf16[160,1280]{1,0:T(8,128)(2,1)}, bf16[160,1280]{1,0:T(8,128)(2,1)}, u32[]{:S(2)}, u32[]{:S(2)}) collective-permute-start(bf16[160,1280]{1,0:T(8,128)(2,1)} %collective-permute-done.13.refs_7_), channel_id=1, source_target_pairs={{0,1},{1,0},{2,3},{3,2},{4,5},{5,4},{6,7},{7,6},{8,9},{9,8},{10,11... | collective-permute-start | bytes 1228808 | tf_op jit(solution)/shard_map/ppermute | solution.py:36
  73.6 23.7 %collective-permute-start = (bf16[2,32,1280]{2,1,0:T(8,128)(2,1)}, bf16[2,32,1280]{2,1,0:T(8,128)(2,1)S(1)}, u32[]{:S(2)}, u32[]{:S(2)}) collective-permute-start(bf16[2,32,1280]{2,1,0:T(8,128)(2,1)} %get-tuple-element.61), channel_id=1, source_target_pairs={{0,1},{1,0},{2,3},{3,2},{4,5},{5,4},{6,7},{7,6}} | collective-permute-start | bytes 491528 | tf_op jit(solution)/shard_map/ppermute | solution.py:406
  75.8 21.6 %collective-permute-start.1 = (bf16[2,32,1280]{2,1,0:T(8,128)(2,1)}, bf16[2,32,1280]{2,1,0:T(8,128)(2,1)S(1)}, u32[]{:S(2)}, u32[]{:S(2)}) collective-permute-start(bf16[2,32,1280]{2,1,0:T(8,128)(2,1)} %get-tuple-element.62), channel_id=1, source_target_pairs={{0,2},{1,3},{2,0},{3,1},{4,6},{5,7},{6,4},{7,5}} | collective-permute-start | bytes 491528 | tf_op jit(solution)/shard_map/ppermute | solution.py:406
  79.2 18.1 %collective-permute-start.2 = (bf16[2,32,1280]{2,1,0:T(8,128)(2,1)}, bf16[2,32,1280]{2,1,0:T(8,128)(2,1)S(1)}, u32[]{:S(2)}, u32[]{:S(2)}) collective-permute-start(bf16[2,32,1280]{2,1,0:T(8,128)(2,1)} %get-tuple-element.63), channel_id=1, source_target_pairs={{0,3},{1,2},{2,1},{3,0},{4,7},{5,6},{6,5},{7,4}} | collective-permute-start | bytes 491528 | tf_op jit(solution)/shard_map/ppermute | solution.py:406
  82.3 1.0 copy-start.10
  83.3 1.0 copy-start.12
  84.3 1.0 copy-start.14
  85.3 1.0 copy-start.16
  86.3 1.0 copy-start.18
  87.3 1.0 copy-start.20
  88.3 1.0 copy-start.22
  90.3 4.4 %copy-start.2 = (bf16[1,320,1280]{2,1,0:T(8,128)(2,1)S(1)}, bf16[1,320,1280]{2,1,0:T(8,128)(2,1)}, u32[]{:S(2)}) copy-start(bf16[1,320,1280]{2,1,0:T(8,128)(2,1)} %param.23) | copy-start | bytes 2457604
  90.3 4.4 %copy-start.3 = (bf16[2,320,128]{2,1,0:T(8,128)(2,1)S(1)}, bf16[2,320,128]{2,1,0:T(8,128)(2,1)}, u32[]{:S(2)}) copy-start(bf16[2,320,128]{2,1,0:T(8,128)(2,1)} %get-tuple-element.92.refs_4_.refs_6_) | copy-start | bytes 491524
  90.3 4.4 %copy-start.5 = (bf16[2,320,128]{2,1,0:T(8,128)(2,1)S(1)}, bf16[2,320,128]{2,1,0:T(8,128)(2,1)}, u32[]{:S(2)}) copy-start(bf16[2,320,128]{2,1,0:T(8,128)(2,1)} %copy-done.4) | copy-start | bytes 491524
  94.1 14.1 %collective-permute-start.24 = (bf16[160,1280]{1,0:T(8,128)(2,1)}, bf16[160,1280]{1,0:T(8,128)(2,1)S(1)}, u32[]{:S(2)}, u32[]{:S(2)}) collective-permute-start(bf16[160,1280]{1,0:T(8,128)(2,1)} %collective-permute-done.22.refs_2_), channel_id=1, source_target_pairs={{0,1},{1,0},{2,3},{3,2},{4,5},{5,4},{6,7},{7,6},{8,9},{9,8},{10,11... | collective-permute-start | bytes 1228808 | tf_op jit(solution)/shard_map/ppermute | solution.py:36
  94.7 13.6 %collective-permute-start.25 = (bf16[160,1280]{1,0:T(8,128)(2,1)}, bf16[160,1280]{1,0:T(8,128)(2,1)S(1)}, u32[]{:S(2)}, u32[]{:S(2)}) collective-permute-start(bf16[160,1280]{1,0:T(8,128)(2,1)} %collective-permute-done.23.refs_3_), channel_id=1, source_target_pairs={{0,1},{1,0},{2,3},{3,2},{4,5},{5,4},{6,7},{7,6},{8,9},{9,8},{10,11... | collective-permute-start | bytes 1228808 | tf_op jit(solution)/shard_map/ppermute | solution.py:36
  94.8 2.6 %copy-start.6 = (bf16[2,32,1280]{2,1,0:T(8,128)(2,1)S(1)}, bf16[2,32,1280]{2,1,0:T(8,128)(2,1)}, u32[]{:S(2)}) copy-start(bf16[2,32,1280]{2,1,0:T(8,128)(2,1)} %get-tuple-element.60.refs_2_) | copy-start | bytes 491524
  94.8 2.6 %copy-start.7 = (f32[1,1280]{1,0:T(1,128)S(1)}, f32[1,1280]{1,0:T(1,128)}, u32[]{:S(2)}) copy-start(f32[1,1280]{1,0:T(1,128)} %refs_5_.9) | copy-start | bytes 15364
  94.8 2.6 %copy-start.8 = (f32[1,1280]{1,0:T(1,128)S(1)}, f32[1,1280]{1,0:T(1,128)}, u32[]{:S(2)}) copy-start(f32[1,1280]{1,0:T(1,128)} %refs_6_.11) | copy-start | bytes 15364
  101.5 9.4 %collective-permute-start.6 = (bf16[128,1280]{1,0:T(8,128)(2,1)S(1)}, bf16[128,1280]{1,0:T(8,128)(2,1)S(1)}, u32[]{:S(2)}, u32[]{:S(2)}) collective-permute-start(bf16[128,1280]{1,0:T(8,128)(2,1)S(1)} %shard_map.120), channel_id=1, source_target_pairs={{0,8},{1,9},{2,10},{3,11},{4,12},{5,13},{6,14},{7,15}} | collective-permute-start | bytes 983048 | tf_op jit(solution)/shard_map/ppermute | solution.py:496
  102.8 5.5 %copy-start.27 = (bf16[2,320,128]{2,1,0:T(8,128)(2,1)S(1)}, bf16[2,320,128]{2,1,0:T(8,128)(2,1)}, u32[]{:S(2)}) copy-start(bf16[2,320,128]{2,1,0:T(8,128)(2,1)} %copy-done.26) | copy-start | bytes 491524
  102.8 5.5 %copy-start.29 = (bf16[2,320,128]{2,1,0:T(8,128)(2,1)S(1)}, bf16[2,320,128]{2,1,0:T(8,128)(2,1)}, u32[]{:S(2)}) copy-start(bf16[2,320,128]{2,1,0:T(8,128)(2,1)} %copy-done.28) | copy-start | bytes 491524
  106.9 10.7 %collective-permute-start.7 = (bf16[128,1280]{1,0:T(8,128)(2,1)S(1)}, bf16[128,1280]{1,0:T(8,128)(2,1)S(1)}, u32[]{:S(2)}, u32[]{:S(2)}) collective-permute-start(bf16[128,1280]{1,0:T(8,128)(2,1)S(1)} %shard_map.121), channel_id=1, source_target_pairs={{0,10},{1,11},{2,8},{3,9},{4,14},{5,15},{6,12},{7,13}} | collective-permute-start | bytes 983048 | tf_op jit(solution)/shard_map/ppermute | solution.py:497
  118.2 0.7 collective-permute-start.26
  119.6 2.7 %copy-start.25 = (bf16[1,4,1,32,1280]{4,3,2,1,0:T(8,128)(2,1)S(1)}, bf16[1,4,1,32,1280]{4,3,2,1,0:T(8,128)(2,1)}, u32[]{:S(2)}) copy-start(bf16[1,4,1,32,1280]{4,3,2,1,0:T(8,128)(2,1)} %param.14) | copy-start | bytes 983044
  119.7 2.7 %copy-start.32 = (s32[4]{0:T(128)S(1)}, s32[4]{0:T(128)}, u32[]{:S(2)}) copy-start(s32[4]{0:T(128)} %order_ref.1) | copy-start | bytes 52
  119.7 0.8 collective-permute-start.27
  121.1 48.2 %collective-permute-start.28 = (bf16[128,1280]{1,0:T(8,128)(2,1)S(1)}, bf16[128,1280]{1,0:T(8,128)(2,1)S(1)}, u32[]{:S(2)}, u32[]{:S(2)}) collective-permute-start(bf16[128,1280]{1,0:T(8,128)(2,1)S(1)} %shard_map.126), channel_id=1, source_target_pairs={{24,0},{25,1},{26,2},{27,3},{28,4},{29,5},{30,6},{31,7}} | collective-permute-start | bytes 983048 | tf_op jit(solution)/shard_map/ppermute | solution.py:527
  123.4 7.6 %collective-permute-start.29 = (bf16[1,32,1280]{2,1,0:T(8,128)(2,1)S(1)}, bf16[1,32,1280]{2,1,0:T(8,128)(2,1)S(1)}, u32[]{:S(2)}, u32[]{:S(2)}) collective-permute-start(bf16[1,32,1280]{2,1,0:T(8,128)(2,1)S(1)} %get-tuple-element.101), channel_id=1, source_target_pairs={{0,1},{1,0},{2,3},{3,2},{4,5},{5,4},{6,7},{7,6}} | collective-permute-start | bytes 245768 | tf_op jit(solution)/shard_map/ppermute | solution.py:406
  125.3 6.7 %collective-permute-start.30 = (bf16[1,32,1280]{2,1,0:T(8,128)(2,1)S(1)}, bf16[1,32,1280]{2,1,0:T(8,128)(2,1)S(1)}, u32[]{:S(2)}, u32[]{:S(2)}) collective-permute-start(bf16[1,32,1280]{2,1,0:T(8,128)(2,1)S(1)} %get-tuple-element.102), channel_id=1, source_target_pairs={{0,2},{1,3},{2,0},{3,1},{4,6},{5,7},{6,4},{7,5}} | collective-permute-start | bytes 245768 | tf_op jit(solution)/shard_map/ppermute | solution.py:406
  128.8 6.2 %collective-permute-start.31 = (bf16[1,32,1280]{2,1,0:T(8,128)(2,1)S(1)}, bf16[1,32,1280]{2,1,0:T(8,128)(2,1)S(1)}, u32[]{:S(2)}, u32[]{:S(2)}) collective-permute-start(bf16[1,32,1280]{2,1,0:T(8,128)(2,1)S(1)} %get-tuple-element.103), channel_id=1, source_target_pairs={{0,3},{1,2},{2,1},{3,0},{4,7},{5,6},{6,5},{7,4}} | collective-permute-start | bytes 245768 | tf_op jit(solution)/shard_map/ppermute | solution.py:406
  176.0 6.8 %collective-permute-start.32 = (bf16[128,1280]{1,0:T(8,128)(2,1)S(1)}, bf16[128,1280]{1,0:T(8,128)(2,1)S(1)}, u32[]{:S(2)}, u32[]{:S(2)}) collective-permute-start(bf16[128,1280]{1,0:T(8,128)(2,1)S(1)} %shard_map.128), channel_id=1, source_target_pairs={{0,8},{1,9},{2,10},{3,11},{4,12},{5,13},{6,14},{7,15}} | collective-permute-start | bytes 983048 | tf_op jit(solution)/shard_map/ppermute | solution.py:527
  183.3 0.7 collective-permute-start.33
  184.8 0.7 collective-permute-start.34
  186.2 2.7 %collective-permute-start.35 = (bf16[128,320]{1,0:T(8,128)(2,1)S(1)}, bf16[128,320]{1,0:T(8,128)(2,1)S(1)}, u32[]{:S(2)}, u32[]{:S(2)}) collective-permute-start(bf16[128,320]{1,0:T(8,128)(2,1)S(1)} %get-tuple-element.112), channel_id=1, source_target_pairs={{24,16},{25,17},{26,18},{27,19},{28,20},{29,21},{30,22},{31,23}} | collective-permute-start | bytes 245768 | tf_op jit(solution)/shard_map/ppermute | solution.py:534
  186.9 2.0 collective-permute-start.36
  187.5 40.0 %collective-permute-start.37 = (bf16[128,320]{1,0:T(8,128)(2,1)S(1)}, bf16[128,320]{1,0:T(8,128)(2,1)S(1)}, u32[]{:S(2)}, u32[]{:S(2)}) collective-permute-start(bf16[128,320]{1,0:T(8,128)(2,1)S(1)} %get-tuple-element.110), channel_id=1, source_target_pairs={{24,0},{25,1},{26,2},{27,3},{28,4},{29,5},{30,6},{31,7}} | collective-permute-start | bytes 245768 | tf_op jit(solution)/shard_map/ppermute | solution.py:534
  227.7 3.3 %collective-permute-start.40 = (bf16[1,32,320]{2,1,0:T(8,128)(2,1)S(1)}, bf16[1,32,320]{2,1,0:T(8,128)(2,1)S(1)}, u32[]{:S(2)}, u32[]{:S(2)}) collective-permute-start(bf16[1,32,320]{2,1,0:T(8,128)(2,1)S(1)} %get-tuple-element.121), channel_id=1, source_target_pairs={{0,3},{1,2},{2,1},{3,0},{4,7},{5,6},{6,5},{7,4},{8,11},{9,10},{10,... | collective-permute-start | bytes 61448 | tf_op jit(solution)/shard_map/ppermute | solution.py:406
  227.7 3.9 %collective-permute-start.39 = (bf16[1,32,320]{2,1,0:T(8,128)(2,1)S(1)}, bf16[1,32,320]{2,1,0:T(8,128)(2,1)S(1)}, u32[]{:S(2)}, u32[]{:S(2)}) collective-permute-start(bf16[1,32,320]{2,1,0:T(8,128)(2,1)S(1)} %get-tuple-element.120), channel_id=1, source_target_pairs={{0,2},{1,3},{2,0},{3,1},{4,6},{5,7},{6,4},{7,5},{8,10},{9,11},{10,... | collective-permute-start | bytes 61448 | tf_op jit(solution)/shard_map/ppermute | solution.py:406
  228.3 3.3 %collective-permute-start.38 = (bf16[1,32,320]{2,1,0:T(8,128)(2,1)S(1)}, bf16[1,32,320]{2,1,0:T(8,128)(2,1)S(1)}, u32[]{:S(2)}, u32[]{:S(2)}) collective-permute-start(bf16[1,32,320]{2,1,0:T(8,128)(2,1)S(1)} %get-tuple-element.119), channel_id=1, source_target_pairs={{0,1},{1,0},{2,3},{3,2},{4,5},{5,4},{6,7},{7,6},{8,9},{9,8},{10,11... | collective-permute-start | bytes 61448 | tf_op jit(solution)/shard_map/ppermute | solution.py:406
  (11 other events, 8.4 us)
where the time goes:
time: 233 us; the launch traced here: 232 us
  waiting for transfers between devices  122 us (52%)
  starting transfers between devices  47.2 us (20%)
  Pallas kernels  38.7 us (17%)
  local copies, waits for them, and re-layouts  22.5 us (10%)
    ppermute x6, waiting for transfers between devices, per_device(): x = [lax.ppermute(x, 'section', [(group, (group + 1) % sections)])]  39.7 us
    ppermute x3, waiting for transfers between devices, per_device(): lax.ppermute(piece, 'section', [(final, other)])  38.7 us
    ppermute x18, waiting for transfers between devices, swapped(): return lax.ppermute(value, axis, [(i, i ^ mask) for i in range(count)])  26.6 us
    ppermute x12, starting transfers between devices, sent(): result.append(lax.ppermute(mine[k], axis, pairs[k]))  19.9 us
    pallas_call x9, Pallas kernels, run_stage(): pl.pallas_call(functools.partial(stage_kernel, cols, head_width, tokens,...  18.7 us
    ppermute x18, starting transfers between devices, swapped(): return lax.ppermute(value, axis, [(i, i ^ mask) for i in range(count)])  16.6 us
    unnamed x69, local copies, waits for them, and re-layouts  15.7 us
    ppermute x12, waiting for transfers between devices, sent(): result.append(lax.ppermute(mine[k], axis, pairs[k]))  9.22 us
  transfers between devices with their start and end apart: 41, of which 15 were waited for; matrix products, arithmetic and copies ran while one was open for 3% of the time, Pallas kernels for 11%

commit v1 on v0

--- a/solution.py
+++ b/solution.py
@@ -103,30 +103,30 @@
     )(flags, *([order] if order is not None else []), source)
 
 
-def cut_kernel(which, flag_ref, qkv_ref, last_ref, *refs):
+def cut_kernel(which, pieces, flag_ref, qkv_ref, last_ref, *refs):
     outs, sems = refs[:-1], refs[-1]
     half = outs[0].shape[0]
     parity = flag_ref[2] if which == 0 else 1 - flag_ref[2]
     rows = pl.ds(pl.multiple_of(parity * half, 16), half)
     copies = []
-    for piece, out in enumerate(outs):
+    for index, (piece, out) in enumerate(zip(pieces, outs)):
         source = qkv_ref.at[piece, rows] if piece < 3 else last_ref.at[rows]
-        copies.append(pltpu.make_async_copy(source, out, sems.at[piece]))
+        copies.append(pltpu.make_async_copy(source, out, sems.at[index]))
     for copy in copies:
         copy.start()
     for copy in copies:
         copy.wait()
 
 
-def cut(flags, which, qkv, last):
+def cut(flags, which, pieces, qkv, last):
     span, width = last.shape
     hbm = pl.BlockSpec(memory_space=pltpu.HBM)
     return pl.pallas_call(
-        functools.partial(cut_kernel, which),
+        functools.partial(cut_kernel, which, pieces),
         in_specs=[pl.BlockSpec(memory_space=pltpu.SMEM), hbm, hbm],
-        out_specs=[pl.BlockSpec(memory_space=pltpu.VMEM)] * 4,
-        out_shape=[jax.ShapeDtypeStruct((span // 2, width), jnp.bfloat16)] * 4,
-        scratch_shapes=[pltpu.SemaphoreType.DMA((4,))],
+        out_specs=[pl.BlockSpec(memory_space=pltpu.VMEM)] * len(pieces),
+        out_shape=[jax.ShapeDtypeStruct((span // 2, width), jnp.bfloat16)] * len(pieces),
+        scratch_shapes=[pltpu.SemaphoreType.DMA((len(pieces),))],
         compiler_params=pltpu.CompilerParams(vmem_limit_bytes=60 * 2**20),
         name="cut",
     )(flags, qkv, last)
@@ -307,7 +307,7 @@
             )
             return carry
 
-        lax.fori_loop(0, rows_total // pair, pair_step, 0, unroll=5)
+        lax.fori_loop(0, rows_total // pair, pair_step, 0, unroll=min(10, rows_total // pair))
 
         piece = 2 * LANES
         for start in range(0, width, piece):
@@ -389,7 +389,7 @@
             moved.append(swapped(piece, axis, mask))
         return moved
 
-    halves = list(cut(flags, 0, own_qkv, own_out))
+    halves = list(cut(flags, 0, (0, 1, 2, 3), own_qkv, own_out))
     halves, own_qkv, own_out, prompt_tokens, latents, fresh_noise = lax.optimization_barrier(
         (halves, own_qkv, own_out, prompt_tokens, latents, fresh_noise)
     )
@@ -420,7 +420,7 @@
 
     def relayed(near, bit):
         if not paired:
-            return exchanged(list(cut(flags, 1, own_qkv, own_out)), "tile", bit)
+            return exchanged(list(cut(flags, 1, (0, 1, 2, 3), own_qkv, own_out)), "tile", bit)
         far = []
         for piece in range(4):
             far.append(swapped(near[piece], "batch", 1))
@@ -460,10 +460,9 @@
     for slot in range(3, tiles):
         bit = 1 << (slot.bit_length() - 1)
         if slot != bit:
-            slots[slot] = [
-                None if index % 4 == 3 else swapped(piece, "tile", slot - bit)
-                for index, piece in enumerate(slots[bit])
-            ]
+            slots[slot] = []
+            for index, piece in enumerate(slots[bit]):
+                slots[slot].append(None if index % 4 == 3 else swapped(piece, "tile", slot - bit))
 
     noises = [None]
     for level in range(1, steps):

time: 233 us -> 229 us (0.983)
  waiting for transfers between devices: 122 us -> 118 us
where the time goes in v1:
time: 229 us; the launch traced here: 228 us
  waiting for transfers between devices  118 us (52%)
  starting transfers between devices  47.2 us (21%)
  Pallas kernels  38.3 us (17%)
  local copies, waits for them, and re-layouts  22.5 us (10%)
    ppermute x6, waiting for transfers between devices, per_device(): x = [lax.ppermute(x, 'section', [(group, (group + 1) % sections)])]  37.8 us
    ppermute x3, waiting for transfers between devices, per_device(): lax.ppermute(piece, 'section', [(final, other)])  36.8 us
    ppermute x18, waiting for transfers between devices, swapped(): return lax.ppermute(value, axis, [(i, i ^ mask) for i in range(count)])  26.6 us
    ppermute x12, starting transfers between devices, sent(): result.append(lax.ppermute(mine[k], axis, pairs[k]))  19.9 us
    pallas_call x9, Pallas kernels, run_stage(): pl.pallas_call(functools.partial(stage_kernel, cols, head_width, tokens,...  18.3 us
    ppermute x18, starting transfers between devices, swapped(): return lax.ppermute(value, axis, [(i, i ^ mask) for i in range(count)])  16.6 us
    unnamed x69, local copies, waits for them, and re-layouts  15.7 us
    ppermute x12, waiting for transfers between devices, sent(): result.append(lax.ppermute(mine[k], axis, pairs[k]))  9.22 us
  transfers between devices with their start and end apart: 41, of which 15 were waited for; matrix products, arithmetic and copies ran while one was open for 3% of the time, Pallas kernels for 11%

profile of v1, /device:TPU:0, one launch (start us, length us, event | category | flops | bytes accessed | tf_op | source)
XLA Modules:
  0.0 228.3 jit_solution(7972613489751117988)
XLA Ops:
  0.6 3.4 %cut.1 = (bf16[160,1280]{1,0:T(8,128)(2,1)}, bf16[160,1280]{1,0:T(8,128)(2,1)}, bf16[160,1280]{1,0:T(8,128)(2,1)}, bf16[160,1280]{1,0:T(8,128)(2,1)}) custom-call(s32[3]{0:T(128)} %pad_add_fusion.flag_ref.refs_0_, bf16[3,320,1280]{2,1,0:T(8,128)(2,1)} %bitcast.44, bf16[320,1280]{1,0:T(8,128)(2,1)} %bitcast.57), custom_call_target="tpu_custom_call" | custom-call | tf_op jit(solution)/shard_map/cut/pallas_call | solution.py:124
  4.6 2.0 copy.13
  6.6 1.6 pad.4.token_ref
  8.2 4.6 %prompts.1 = bf16[4,640,128]{2,1,0:T(8,128)(2,1)} custom-call(bf16[4,128,2048]{2,1,0:T(8,128)(2,1)} %pad.4.token_ref, bf16[640,2048]{1,0:T(8,128)(2,1)} %bitcast.60), custom_call_target="tpu_custom_call" | custom-call | tf_op jit(solution)/shard_map/prompts/pallas_call | solution.py:54
  12.8 2.0 dynamic-slice_bitcast_fusion
  14.7 2.5 %collective-permute-start.20 = (bf16[2,320,128]{2,1,0:T(8,128)(2,1)S(1)}, bf16[2,320,128]{2,1,0:T(8,128)(2,1)S(1)}, u32[]{:S(2)}, u32[]{:S(2)}) collective-permute-start(bf16[2,320,128]{2,1,0:T(8,128)(2,1)S(1)} %get-tuple-element.106.refs_6_), channel_id=1, source_target_pairs={{0,2},{1,3},{2,0},{3,1},{4,6},{5,7},{6,4},{7,5},{8,10},{9,11},{10,... | collective-permute-start | bytes 491528 | tf_op jit(solution)/shard_map/ppermute | solution.py:406
  17.6 1.9 collective-permute-start.8
  19.5 2.8 %collective-permute-done.20.refs_8_ = bf16[2,320,128]{2,1,0:T(8,128)(2,1)S(1)} collective-permute-done((bf16[2,320,128]{2,1,0:T(8,128)(2,1)S(1)}, bf16[2,320,128]{2,1,0:T(8,128)(2,1)S(1)}, u32[]{:S(2)}, u32[]{:S(2)}) %collective-permute-start.20) | collective-permute-done | bytes 163872 | tf_op jit(solution)/shard_map/ppermute | solution.py:406
  23.0 2.0 collective-permute-start.9
  26.0 1.5 collective-permute-start.10
  28.2 6.4 %collective-permute-done.8.refs_2_ = bf16[160,1280]{1,0:T(8,128)(2,1)S(1)} collective-permute-done((bf16[160,1280]{1,0:T(8,128)(2,1)}, bf16[160,1280]{1,0:T(8,128)(2,1)S(1)}, u32[]{:S(2)}, u32[]{:S(2)}) %collective-permute-start.8) | collective-permute-done | bytes 409632 | tf_op jit(solution)/shard_map/ppermute | solution.py:36
  34.6 2.0 collective-permute-start.11
  36.6 6.8 %collective-permute-done.9.refs_3_ = bf16[160,1280]{1,0:T(8,128)(2,1)S(1)} collective-permute-done((bf16[160,1280]{1,0:T(8,128)(2,1)}, bf16[160,1280]{1,0:T(8,128)(2,1)S(1)}, u32[]{:S(2)}, u32[]{:S(2)}) %collective-permute-start.9) | collective-permute-done | bytes 409632 | tf_op jit(solution)/shard_map/ppermute | solution.py:36
  43.4 2.0 collective-permute-start.12
  45.4 6.8 %collective-permute-done.10.refs_4_ = bf16[160,1280]{1,0:T(8,128)(2,1)S(1)} collective-permute-done((bf16[160,1280]{1,0:T(8,128)(2,1)}, bf16[160,1280]{1,0:T(8,128)(2,1)S(1)}, u32[]{:S(2)}, u32[]{:S(2)}) %collective-permute-start.10) | collective-permute-done | bytes 409632 | tf_op jit(solution)/shard_map/ppermute | solution.py:36
  52.2 2.0 collective-permute-start.13
  54.1 6.7 %collective-permute-done.22.refs_2_ = bf16[160,1280]{1,0:T(8,128)(2,1)} collective-permute-done((bf16[160,1280]{1,0:T(8,128)(2,1)}, bf16[160,1280]{1,0:T(8,128)(2,1)}, u32[]{:S(2)}, u32[]{:S(2)}) %collective-permute-start.22) | collective-permute-done | bytes 409632 | tf_op jit(solution)/shard_map/ppermute | solution.py:36
  60.8 0.7 copy-done.9
  62.2 0.8 copy-done.11
  62.9 0.7 copy-done.13
  64.2 0.7 copy-done.15
  65.4 0.8 copy-done.19
  66.3 1.7 collective-permute-start.23
  68.0 0.8 copy-done.21
  69.0 0.8 copy-done.23
  70.1 2.7 %shard_map.118 = (bf16[2,32,1280]{2,1,0:T(8,128)(2,1)}, bf16[2,32,1280]{2,1,0:T(8,128)(2,1)}, bf16[2,32,1280]{2,1,0:T(8,128)(2,1)}, bf16[2,32,1280]{2,1,0:T(8,128)(2,1)}) custom-call(s32[3]{0:T(128)} %pad_add_fusion.flag_ref.refs_0_, bf16[128,1280]{1,0:T(8,128)(2,1)} %bitcast.63), custom_call_target="tpu_custom_call" | custom-call | tf_op jit(solution)/shard_map/pallas_call | solution.py:96
  72.8 0.8 copy.17
  73.6 2.1 collective-permute-start
  75.8 3.4 %collective-permute-start.1 = (bf16[2,32,1280]{2,1,0:T(8,128)(2,1)}, bf16[2,32,1280]{2,1,0:T(8,128)(2,1)S(1)}, u32[]{:S(2)}, u32[]{:S(2)}) collective-permute-start(bf16[2,32,1280]{2,1,0:T(8,128)(2,1)} %get-tuple-element.62), channel_id=1, source_target_pairs={{0,2},{1,3},{2,0},{3,1},{4,6},{5,7},{6,4},{7,5}} | collective-permute-start | bytes 491528 | tf_op jit(solution)/shard_map/ppermute | solution.py:406
  79.2 2.0 collective-permute-start.2
  81.3 1.0 slice_bitcast_fusion
  82.3 1.0 copy-done.10
  83.3 1.0 copy-done.12
  84.3 1.0 copy-done.14
  85.3 1.0 copy-done.16
  86.3 1.0 copy-done.18
  87.3 1.0 copy-done.20
  88.3 1.0 copy-done.22
  89.3 1.0 copy-done.24
  90.3 3.8 %shard_map.122.refs_9_.refs_8_.refs_12_ = bf16[3,1280,1280]{2,1,0:T(8,128)(2,1)S(1)} custom-call(s32[3]{0:T(128)S(1)} %copy-done.30, bf16[3,320,1280]{2,1,0:T(8,128)(2,1)S(1)} %bitcast.46, bf16[3,320,1280]{2,1,0:T(8,128)(2,1)} %collective-permute-done.3.refs_1_, bf16[160,1280]{1,0:T(8,128)(2,1)S(1)} %copy-done.10, bf16[160,1280]{1,0:T(8,128)(2,1)S(1)} %copy-done.12, ...), custom_call_target="tpu_custom_call" | custom-call | tf_op jit(solution)/shard_map/pallas_call | solution.py:172
  94.8 2.5 %shard_map.119 = (bf16[3,640,1280]{2,1,0:T(8,128)(2,1)S(1)}, bf16[1,640,1280]{2,1,0:T(8,128)(2,1)S(1)}, bf16[2,640,128]{2,1,0:T(8,128)(2,1)S(1)}, bf16[2,640,128]{2,1,0:T(8,128)(2,1)S(1)}) custom-call(s32[3]{0:T(128)S(1)} %copy-done.30, bf16[3,320,1280]{2,1,0:T(8,128)(2,1)S(1)} %bitcast.47, bf16[3,320,1280]{2,1,0:T(8,128)(2,1)} %collective-permute-done.3.refs_1_, ...), custom_call_target="tpu_custom_call" | custom-call | tf_op jit(solution)/shard_map/pallas_call | solution.py:172
  97.4 4.1 %shard_map.120 = bf16[128,1280]{1,0:T(8,128)(2,1)S(1)} custom-call(s32[3]{0:T(128)S(1)} %copy-done.30, s32[2]{0:T(128)S(1)} %copy-done.31, bf16[2,32,1280]{2,1,0:T(8,128)(2,1)S(1)} %copy-done.6, bf16[2,32,1280]{2,1,0:T(8,128)(2,1)S(1)} %collective-permute-done.refs_3_, bf16[2,32,1280]{2,1,0:T(8,128)(2,1)S(1)} %collective-permute-done.1.refs_4_, ...), custom_call_target="tpu_custom_call" | custom-call | tf_op jit(solution)/shard_map/pallas_call | solution.py:331
  101.5 1.3 collective-permute-start.6
  102.8 4.1 %shard_map.121 = bf16[128,1280]{1,0:T(8,128)(2,1)S(1)} custom-call(s32[3]{0:T(128)S(1)} %copy-done.30, s32[2]{0:T(128)S(1)} %copy-done.31, bf16[2,32,1280]{2,1,0:T(8,128)(2,1)S(1)} %copy-done.6, bf16[2,32,1280]{2,1,0:T(8,128)(2,1)S(1)} %collective-permute-done.refs_3_, bf16[2,32,1280]{2,1,0:T(8,128)(2,1)S(1)} %collective-permute-done.1.refs_4_, ...), custom_call_target="tpu_custom_call" | custom-call | tf_op jit(solution)/shard_map/pallas_call | solution.py:331
  106.9 1.3 collective-permute-start.7
  108.3 2.0 shard_map.123
  110.9 6.8 %collective-permute-done.7.refs_3_ = bf16[128,1280]{1,0:T(8,128)(2,1)S(1)} collective-permute-done((bf16[128,1280]{1,0:T(8,128)(2,1)S(1)}, bf16[128,1280]{1,0:T(8,128)(2,1)S(1)}, u32[]{:S(2)}, u32[]{:S(2)}) %collective-permute-start.7) | collective-permute-done | bytes 327712 | tf_op jit(solution)/shard_map/ppermute | solution.py:496
  119.7 0.8 collective-permute-start.27
  121.1 1.3 collective-permute-start.28
  122.4 1.0 shard_map.127
  123.4 1.9 collective-permute-start.29
  125.3 3.4 %collective-permute-start.30 = (bf16[1,32,1280]{2,1,0:T(8,128)(2,1)S(1)}, bf16[1,32,1280]{2,1,0:T(8,128)(2,1)S(1)}, u32[]{:S(2)}, u32[]{:S(2)}) collective-permute-start(bf16[1,32,1280]{2,1,0:T(8,128)(2,1)S(1)} %get-tuple-element.102), channel_id=1, source_target_pairs={{0,2},{1,3},{2,0},{3,1},{4,6},{5,7},{6,4},{7,5}} | collective-permute-start | bytes 245768 | tf_op jit(solution)/shard_map/ppermute | solution.py:406
  128.8 2.2 collective-permute-start.31
  131.0 1.0 collective-permute-done.30.refs_5_
  132.1 2.9 %collective-permute-done.31.refs_6_ = bf16[1,32,1280]{2,1,0:T(8,128)(2,1)S(1)} collective-permute-done((bf16[1,32,1280]{2,1,0:T(8,128)(2,1)S(1)}, bf16[1,32,1280]{2,1,0:T(8,128)(2,1)S(1)}, u32[]{:S(2)}, u32[]{:S(2)}) %collective-permute-start.31) | collective-permute-done | bytes 81952 | tf_op jit(solution)/shard_map/ppermute | solution.py:406
  135.0 32.3 %collective-permute-done.28.refs_2_ = bf16[128,1280]{1,0:T(8,128)(2,1)S(1)} collective-permute-done((bf16[128,1280]{1,0:T(8,128)(2,1)S(1)}, bf16[128,1280]{1,0:T(8,128)(2,1)S(1)}, u32[]{:S(2)}, u32[]{:S(2)}) %collective-permute-start.28) | collective-permute-done | bytes 327712 | tf_op jit(solution)/shard_map/ppermute | solution.py:526
  167.3 6.3 %shard_map.128 = bf16[128,1280]{1,0:T(8,128)(2,1)S(1)} custom-call(s32[3]{0:T(128)S(1)} %copy-done.30, s32[2]{0:T(128)S(1)} %copy-done.31, bf16[128,1280]{1,0:T(8,128)(2,1)S(1)} %collective-permute-done.28.refs_2_, bf16[1,32,1280]{2,1,0:T(8,128)(2,1)S(1)} %get-tuple-element.100.refs_3_, bf16[1,32,1280]{2,1,0:T(8,128)(2,1)S(1)} %collective-permute-done.29.refs_4_, ...), custom_call_target="tpu_custom_call" | custom-call | tf_op jit(solution)/shard_map/pallas_call | solution.py:331
  173.7 1.3 collective-permute-start.32
  175.0 5.5 %collective-permute-done.32.refs_2_ = bf16[128,1280]{1,0:T(8,128)(2,1)S(1)} collective-permute-done((bf16[128,1280]{1,0:T(8,128)(2,1)S(1)}, bf16[128,1280]{1,0:T(8,128)(2,1)S(1)}, u32[]{:S(2)}, u32[]{:S(2)}) %collective-permute-start.32) | collective-permute-done | bytes 327712 | tf_op jit(solution)/shard_map/ppermute | solution.py:526
  183.0 0.8 shard_map.131
  185.3 1.3 collective-permute-start.37
  186.6 36.8 %collective-permute-done.37 = bf16[128,320]{1,0:T(8,128)(2,1)S(1)} collective-permute-done((bf16[128,320]{1,0:T(8,128)(2,1)S(1)}, bf16[128,320]{1,0:T(8,128)(2,1)S(1)}, u32[]{:S(2)}, u32[]{:S(2)}) %collective-permute-start.37) | collective-permute-done | bytes 81952 | tf_op jit(solution)/shard_map/ppermute | solution.py:533
  224.1 1.3 collective-permute-start.38
  225.5 1.4 collective-permute-done.40
  (121 shorter events, 15.9 us)
Async XLA Ops:
  0.0 65.2 %copy-start = (bf16[1,320,1280]{2,1,0:T(8,128)(2,1)S(1)}, bf16[1,320,1280]{2,1,0:T(8,128)(2,1)}, u32[]{:S(2)}) copy-start(bf16[1,320,1280]{2,1,0:T(8,128)(2,1)} %param.17) | copy-start | bytes 2457604
  0.0 4.0 %copy-start.1 = (bf16[1,1280,3,320]{1,3,2,0:T(8,128)(2,1)S(1)}, bf16[1,1280,3,320]{1,3,2,0:T(8,128)(2,1)}, u32[]{:S(2)}) copy-start(bf16[1,1280,3,320]{1,3,2,0:T(8,128)(2,1)} %param.21) | copy-start | bytes 7372804
  4.0 75.2 %collective-permute-start.3 = (bf16[3,320,1280]{2,1,0:T(8,128)(2,1)S(1)}, bf16[3,320,1280]{2,1,0:T(8,128)(2,1)}, u32[]{:S(2)}, u32[]{:S(2)}) collective-permute-start(bf16[3,320,1280]{2,1,0:T(8,128)(2,1)S(1)} %bitcast.45), channel_id=1, source_target_pairs={{0,1},{1,0},{2,3},{3,2},{4,5},{5,4},{6,7},{7,6},{8,9},{9,8},{10,11... | collective-permute-start | bytes 7372808 | tf_op jit(solution)/shard_map/ppermute | solution.py:36
  8.2 53.4 %copy-start.31 = (s32[2]{0:T(128)S(1)}, s32[2]{0:T(128)}, u32[]{:S(2)}) copy-start(s32[2]{0:T(128)} %refs_1_.17) | copy-start | bytes 28
  12.8 69.5 %copy-start.30 = (s32[3]{0:T(128)S(1)}, s32[3]{0:T(128)}, u32[]{:S(2)}) copy-start(s32[3]{0:T(128)} %pad_add_fusion.flag_ref.refs_0_) | copy-start | bytes 40
  14.7 50.4 %copy-start.4 = (bf16[2,320,128]{2,1,0:T(8,128)(2,1)}, bf16[2,320,128]{2,1,0:T(8,128)(2,1)S(1)}, u32[]{:S(2)}) copy-start(bf16[2,320,128]{2,1,0:T(8,128)(2,1)S(1)} %get-tuple-element.106.refs_6_) | copy-start | bytes 491524
  14.7 7.6 %collective-permute-start.20 = (bf16[2,320,128]{2,1,0:T(8,128)(2,1)S(1)}, bf16[2,320,128]{2,1,0:T(8,128)(2,1)S(1)}, u32[]{:S(2)}, u32[]{:S(2)}) collective-permute-start(bf16[2,320,128]{2,1,0:T(8,128)(2,1)S(1)} %get-tuple-element.106.refs_6_), channel_id=1, source_target_pairs={{0,2},{1,3},{2,0},{3,1},{4,6},{5,7},{6,4},{7,5},{8,10},{9,11},{10,... | collective-permute-start | bytes 491528 | tf_op jit(solution)/shard_map/ppermute | solution.py:406
  17.3 8.1 %collective-permute-start.21 = (bf16[2,320,128]{2,1,0:T(8,128)(2,1)S(1)}, bf16[2,320,128]{2,1,0:T(8,128)(2,1)S(1)}, u32[]{:S(2)}, u32[]{:S(2)}) collective-permute-start(bf16[2,320,128]{2,1,0:T(8,128)(2,1)S(1)} %get-tuple-element.105), channel_id=1, source_target_pairs={{0,3},{1,2},{2,1},{3,0},{4,7},{5,6},{6,5},{7,4},{8,11},{9,10},{10,... | collective-permute-start | bytes 491528 | tf_op jit(solution)/shard_map/ppermute | solution.py:406
  17.4 10.1 %collective-permute-start.5 = (bf16[2,2,320,128]{3,2,1,0:T(8,128)(2,1)S(1)}, bf16[2,2,320,128]{3,2,1,0:T(8,128)(2,1)S(1)}, u32[]{:S(2)}, u32[]{:S(2)}) collective-permute-start(bf16[2,2,320,128]{3,2,1,0:T(8,128)(2,1)S(1)} %pad_maximum_fusion), channel_id=1, source_target_pairs={{0,1},{1,0},{2,3},{3,2},{4,5},{5,4},{6,7},{7,6},{8,9},{9,8},{10,11... | collective-permute-start | bytes 983048 | tf_op jit(solution)/shard_map/ppermute | solution.py:406
  17.6 17.0 %collective-permute-start.8 = (bf16[160,1280]{1,0:T(8,128)(2,1)}, bf16[160,1280]{1,0:T(8,128)(2,1)S(1)}, u32[]{:S(2)}, u32[]{:S(2)}) collective-permute-start(bf16[160,1280]{1,0:T(8,128)(2,1)} %get-tuple-element.71), channel_id=1, source_target_pairs={{0,2},{1,3},{2,0},{3,1},{4,6},{5,7},{6,4},{7,5},{8,10},{9,11},{10,... | collective-permute-start | bytes 1228808 | tf_op jit(solution)/shard_map/ppermute | solution.py:36
  23.0 20.4 %collective-permute-start.9 = (bf16[160,1280]{1,0:T(8,128)(2,1)}, bf16[160,1280]{1,0:T(8,128)(2,1)S(1)}, u32[]{:S(2)}, u32[]{:S(2)}) collective-permute-start(bf16[160,1280]{1,0:T(8,128)(2,1)} %get-tuple-element.72), channel_id=1, source_target_pairs={{0,2},{1,3},{2,0},{3,1},{4,6},{5,7},{6,4},{7,5},{8,10},{9,11},{10,... | collective-permute-start | bytes 1228808 | tf_op jit(solution)/shard_map/ppermute | solution.py:36
  26.0 26.1 %collective-permute-start.10 = (bf16[160,1280]{1,0:T(8,128)(2,1)}, bf16[160,1280]{1,0:T(8,128)(2,1)S(1)}, u32[]{:S(2)}, u32[]{:S(2)}) collective-permute-start(bf16[160,1280]{1,0:T(8,128)(2,1)} %get-tuple-element.73), channel_id=1, source_target_pairs={{0,2},{1,3},{2,0},{3,1},{4,6},{5,7},{6,4},{7,5},{8,10},{9,11},{10,... | collective-permute-start | bytes 1228808 | tf_op jit(solution)/shard_map/ppermute | solution.py:36
  27.5 33.3 %collective-permute-start.22 = (bf16[160,1280]{1,0:T(8,128)(2,1)}, bf16[160,1280]{1,0:T(8,128)(2,1)}, u32[]{:S(2)}, u32[]{:S(2)}) collective-permute-start(bf16[160,1280]{1,0:T(8,128)(2,1)} %get-tuple-element.76), channel_id=1, source_target_pairs={{0,2},{1,3},{2,0},{3,1},{4,6},{5,7},{6,4},{7,5},{8,10},{9,11},{10,... | collective-permute-start | bytes 1228808 | tf_op jit(solution)/shard_map/ppermute | solution.py:36
  34.6 27.0 %collective-permute-start.11 = (bf16[160,1280]{1,0:T(8,128)(2,1)S(1)}, bf16[160,1280]{1,0:T(8,128)(2,1)S(1)}, u32[]{:S(2)}, u32[]{:S(2)}) collective-permute-start(bf16[160,1280]{1,0:T(8,128)(2,1)S(1)} %collective-permute-done.8.refs_2_), channel_id=1, source_target_pairs={{0,4},{4,0},{1,5},{5,1},{2,6},{6,2},{3,7},{7,3},{8,12},{12,8},{9,1... | collective-permute-start | bytes 1228808 | tf_op jit(solution)/shard_map/ppermute | solution.py:36
  43.4 19.5 %collective-permute-start.12 = (bf16[160,1280]{1,0:T(8,128)(2,1)S(1)}, bf16[160,1280]{1,0:T(8,128)(2,1)}, u32[]{:S(2)}, u32[]{:S(2)}) collective-permute-start(bf16[160,1280]{1,0:T(8,128)(2,1)S(1)} %collective-permute-done.9.refs_3_), channel_id=1, source_target_pairs={{0,4},{4,0},{1,5},{5,1},{2,6},{6,2},{3,7},{7,3},{8,12},{12,8},{9,1... | collective-permute-start | bytes 1228808 | tf_op jit(solution)/shard_map/ppermute | solution.py:36
  52.2 11.5 %collective-permute-start.13 = (bf16[160,1280]{1,0:T(8,128)(2,1)S(1)}, bf16[160,1280]{1,0:T(8,128)(2,1)}, u32[]{:S(2)}, u32[]{:S(2)}) collective-permute-start(bf16[160,1280]{1,0:T(8,128)(2,1)S(1)} %collective-permute-done.10.refs_4_), channel_id=1, source_target_pairs={{0,4},{4,0},{1,5},{5,1},{2,6},{6,2},{3,7},{7,3},{8,12},{12,8},{9,1... | collective-permute-start | bytes 1228808 | tf_op jit(solution)/shard_map/ppermute | solution.py:36
  60.8 4.2 %collective-permute-start.14 = (bf16[160,1280]{1,0:T(8,128)(2,1)S(1)}, bf16[160,1280]{1,0:T(8,128)(2,1)S(1)}, u32[]{:S(2)}, u32[]{:S(2)}) collective-permute-start(bf16[160,1280]{1,0:T(8,128)(2,1)S(1)} %collective-permute-done.8.refs_2_), channel_id=1, source_target_pairs={{0,1},{1,0},{2,3},{3,2},{4,5},{5,4},{6,7},{7,6},{8,9},{9,8},{10,11... | collective-permute-start | bytes 1228808 | tf_op jit(solution)/shard_map/ppermute | solution.py:36
  61.6 3.8 %collective-permute-start.15 = (bf16[160,1280]{1,0:T(8,128)(2,1)S(1)}, bf16[160,1280]{1,0:T(8,128)(2,1)S(1)}, u32[]{:S(2)}, u32[]{:S(2)}) collective-permute-start(bf16[160,1280]{1,0:T(8,128)(2,1)S(1)} %collective-permute-done.9.refs_3_), channel_id=1, source_target_pairs={{0,1},{1,0},{2,3},{3,2},{4,5},{5,4},{6,7},{7,6},{8,9},{9,8},{10,11... | collective-permute-start | bytes 1228808 | tf_op jit(solution)/shard_map/ppermute | solution.py:36
  62.9 5.1 %collective-permute-start.16 = (bf16[160,1280]{1,0:T(8,128)(2,1)S(1)}, bf16[160,1280]{1,0:T(8,128)(2,1)S(1)}, u32[]{:S(2)}, u32[]{:S(2)}) collective-permute-start(bf16[160,1280]{1,0:T(8,128)(2,1)S(1)} %collective-permute-done.10.refs_4_), channel_id=1, source_target_pairs={{0,1},{1,0},{2,3},{3,2},{4,5},{5,4},{6,7},{7,6},{8,9},{9,8},{10,11... | collective-permute-start | bytes 1228808 | tf_op jit(solution)/shard_map/ppermute | solution.py:36
  63.7 5.3 %collective-permute-start.17 = (bf16[160,1280]{1,0:T(8,128)(2,1)S(1)}, bf16[160,1280]{1,0:T(8,128)(2,1)S(1)}, u32[]{:S(2)}, u32[]{:S(2)}) collective-permute-start(bf16[160,1280]{1,0:T(8,128)(2,1)S(1)} %collective-permute-done.11.refs_5_), channel_id=1, source_target_pairs={{0,1},{1,0},{2,3},{3,2},{4,5},{5,4},{6,7},{7,6},{8,9},{9,8},{10,11... | collective-permute-start | bytes 1228808 | tf_op jit(solution)/shard_map/ppermute | solution.py:36
  65.1 3.9 %copy-start.17 = (bf16[160,1280]{1,0:T(8,128)(2,1)}, bf16[160,1280]{1,0:T(8,128)(2,1)S(1)}, u32[]{:S(2)}) copy-start(bf16[160,1280]{1,0:T(8,128)(2,1)S(1)} %collective-permute-done.14.refs_8_) | copy-start | bytes 1228804
  65.1 29.6 %collective-permute-start.4 = (bf16[1,320,1280]{2,1,0:T(8,128)(2,1)}, bf16[1,320,1280]{2,1,0:T(8,128)(2,1)S(1)}, u32[]{:S(2)}, u32[]{:S(2)}) collective-permute-start(bf16[1,320,1280]{2,1,0:T(8,128)(2,1)} %param.23), channel_id=1, source_target_pairs={{0,1},{1,0},{2,3},{3,2},{4,5},{5,4},{6,7},{7,6},{8,9},{9,8},{10,11... | collective-permute-start | bytes 2457608 | tf_op jit(solution)/shard_map/ppermute | solution.py:36
  66.3 27.9 %collective-permute-start.23 = (bf16[160,1280]{1,0:T(8,128)(2,1)}, bf16[160,1280]{1,0:T(8,128)(2,1)}, u32[]{:S(2)}, u32[]{:S(2)}) collective-permute-start(bf16[160,1280]{1,0:T(8,128)(2,1)} %collective-permute-done.22.refs_2_), channel_id=1, source_target_pairs={{0,4},{4,0},{1,5},{5,1},{2,6},{6,2},{3,7},{7,3},{8,12},{12,8},{9,1... | collective-permute-start | bytes 1228808 | tf_op jit(solution)/shard_map/ppermute | solution.py:36
  68.8 4.9 %collective-permute-start.18 = (bf16[160,1280]{1,0:T(8,128)(2,1)}, bf16[160,1280]{1,0:T(8,128)(2,1)}, u32[]{:S(2)}, u32[]{:S(2)}) collective-permute-start(bf16[160,1280]{1,0:T(8,128)(2,1)} %collective-permute-done.12.refs_6_), channel_id=1, source_target_pairs={{0,1},{1,0},{2,3},{3,2},{4,5},{5,4},{6,7},{7,6},{8,9},{9,8},{10,11... | collective-permute-start | bytes 1228808 | tf_op jit(solution)/shard_map/ppermute | solution.py:36
  69.8 6.0 %collective-permute-start.19 = (bf16[160,1280]{1,0:T(8,128)(2,1)}, bf16[160,1280]{1,0:T(8,128)(2,1)}, u32[]{:S(2)}, u32[]{:S(2)}) collective-permute-start(bf16[160,1280]{1,0:T(8,128)(2,1)} %collective-permute-done.13.refs_7_), channel_id=1, source_target_pairs={{0,1},{1,0},{2,3},{3,2},{4,5},{5,4},{6,7},{7,6},{8,9},{9,8},{10,11... | collective-permute-start | bytes 1228808 | tf_op jit(solution)/shard_map/ppermute | solution.py:36
  73.6 23.7 %collective-permute-start = (bf16[2,32,1280]{2,1,0:T(8,128)(2,1)}, bf16[2,32,1280]{2,1,0:T(8,128)(2,1)S(1)}, u32[]{:S(2)}, u32[]{:S(2)}) collective-permute-start(bf16[2,32,1280]{2,1,0:T(8,128)(2,1)} %get-tuple-element.61), channel_id=1, source_target_pairs={{0,1},{1,0},{2,3},{3,2},{4,5},{5,4},{6,7},{7,6}} | collective-permute-start | bytes 491528 | tf_op jit(solution)/shard_map/ppermute | solution.py:406
  75.8 21.6 %collective-permute-start.1 = (bf16[2,32,1280]{2,1,0:T(8,128)(2,1)}, bf16[2,32,1280]{2,1,0:T(8,128)(2,1)S(1)}, u32[]{:S(2)}, u32[]{:S(2)}) collective-permute-start(bf16[2,32,1280]{2,1,0:T(8,128)(2,1)} %get-tuple-element.62), channel_id=1, source_target_pairs={{0,2},{1,3},{2,0},{3,1},{4,6},{5,7},{6,4},{7,5}} | collective-permute-start | bytes 491528 | tf_op jit(solution)/shard_map/ppermute | solution.py:406
  79.2 18.1 %collective-permute-start.2 = (bf16[2,32,1280]{2,1,0:T(8,128)(2,1)}, bf16[2,32,1280]{2,1,0:T(8,128)(2,1)S(1)}, u32[]{:S(2)}, u32[]{:S(2)}) collective-permute-start(bf16[2,32,1280]{2,1,0:T(8,128)(2,1)} %get-tuple-element.63), channel_id=1, source_target_pairs={{0,3},{1,2},{2,1},{3,0},{4,7},{5,6},{6,5},{7,4}} | collective-permute-start | bytes 491528 | tf_op jit(solution)/shard_map/ppermute | solution.py:406
  82.3 1.0 copy-start.10
  83.3 1.0 copy-start.12
  84.3 1.0 copy-start.14
  85.3 1.0 copy-start.16
  86.3 1.0 copy-start.18
  87.3 1.0 copy-start.20
  88.3 1.0 copy-start.22
  90.3 4.4 %copy-start.2 = (bf16[1,320,1280]{2,1,0:T(8,128)(2,1)S(1)}, bf16[1,320,1280]{2,1,0:T(8,128)(2,1)}, u32[]{:S(2)}) copy-start(bf16[1,320,1280]{2,1,0:T(8,128)(2,1)} %param.23) | copy-start | bytes 2457604
  90.3 4.4 %copy-start.3 = (bf16[2,320,128]{2,1,0:T(8,128)(2,1)S(1)}, bf16[2,320,128]{2,1,0:T(8,128)(2,1)}, u32[]{:S(2)}) copy-start(bf16[2,320,128]{2,1,0:T(8,128)(2,1)} %get-tuple-element.92.refs_4_.refs_6_) | copy-start | bytes 491524
  90.3 4.4 %copy-start.5 = (bf16[2,320,128]{2,1,0:T(8,128)(2,1)S(1)}, bf16[2,320,128]{2,1,0:T(8,128)(2,1)}, u32[]{:S(2)}) copy-start(bf16[2,320,128]{2,1,0:T(8,128)(2,1)} %copy-done.4) | copy-start | bytes 491524
  94.1 14.1 %collective-permute-start.24 = (bf16[160,1280]{1,0:T(8,128)(2,1)}, bf16[160,1280]{1,0:T(8,128)(2,1)S(1)}, u32[]{:S(2)}, u32[]{:S(2)}) collective-permute-start(bf16[160,1280]{1,0:T(8,128)(2,1)} %collective-permute-done.22.refs_2_), channel_id=1, source_target_pairs={{0,1},{1,0},{2,3},{3,2},{4,5},{5,4},{6,7},{7,6},{8,9},{9,8},{10,11... | collective-permute-start | bytes 1228808 | tf_op jit(solution)/shard_map/ppermute | solution.py:36
  94.7 13.6 %collective-permute-start.25 = (bf16[160,1280]{1,0:T(8,128)(2,1)}, bf16[160,1280]{1,0:T(8,128)(2,1)S(1)}, u32[]{:S(2)}, u32[]{:S(2)}) collective-permute-start(bf16[160,1280]{1,0:T(8,128)(2,1)} %collective-permute-done.23.refs_3_), channel_id=1, source_target_pairs={{0,1},{1,0},{2,3},{3,2},{4,5},{5,4},{6,7},{7,6},{8,9},{9,8},{10,11... | collective-permute-start | bytes 1228808 | tf_op jit(solution)/shard_map/ppermute | solution.py:36
  94.8 2.6 %copy-start.6 = (bf16[2,32,1280]{2,1,0:T(8,128)(2,1)S(1)}, bf16[2,32,1280]{2,1,0:T(8,128)(2,1)}, u32[]{:S(2)}) copy-start(bf16[2,32,1280]{2,1,0:T(8,128)(2,1)} %get-tuple-element.60.refs_2_) | copy-start | bytes 491524
  94.8 2.6 %copy-start.7 = (f32[1,1280]{1,0:T(1,128)S(1)}, f32[1,1280]{1,0:T(1,128)}, u32[]{:S(2)}) copy-start(f32[1,1280]{1,0:T(1,128)} %refs_5_.9) | copy-start | bytes 15364
  94.8 2.6 %copy-start.8 = (f32[1,1280]{1,0:T(1,128)S(1)}, f32[1,1280]{1,0:T(1,128)}, u32[]{:S(2)}) copy-start(f32[1,1280]{1,0:T(1,128)} %refs_6_.11) | copy-start | bytes 15364
  101.5 9.4 %collective-permute-start.6 = (bf16[128,1280]{1,0:T(8,128)(2,1)S(1)}, bf16[128,1280]{1,0:T(8,128)(2,1)S(1)}, u32[]{:S(2)}, u32[]{:S(2)}) collective-permute-start(bf16[128,1280]{1,0:T(8,128)(2,1)S(1)} %shard_map.120), channel_id=1, source_target_pairs={{0,8},{1,9},{2,10},{3,11},{4,12},{5,13},{6,14},{7,15}} | collective-permute-start | bytes 983048 | tf_op jit(solution)/shard_map/ppermute | solution.py:495
  102.8 5.5 %copy-start.27 = (bf16[2,320,128]{2,1,0:T(8,128)(2,1)S(1)}, bf16[2,320,128]{2,1,0:T(8,128)(2,1)}, u32[]{:S(2)}) copy-start(bf16[2,320,128]{2,1,0:T(8,128)(2,1)} %copy-done.26) | copy-start | bytes 491524
  102.8 5.5 %copy-start.29 = (bf16[2,320,128]{2,1,0:T(8,128)(2,1)S(1)}, bf16[2,320,128]{2,1,0:T(8,128)(2,1)}, u32[]{:S(2)}) copy-start(bf16[2,320,128]{2,1,0:T(8,128)(2,1)} %copy-done.28) | copy-start | bytes 491524
  106.9 10.7 %collective-permute-start.7 = (bf16[128,1280]{1,0:T(8,128)(2,1)S(1)}, bf16[128,1280]{1,0:T(8,128)(2,1)S(1)}, u32[]{:S(2)}, u32[]{:S(2)}) collective-permute-start(bf16[128,1280]{1,0:T(8,128)(2,1)S(1)} %shard_map.121), channel_id=1, source_target_pairs={{0,10},{1,11},{2,8},{3,9},{4,14},{5,15},{6,12},{7,13}} | collective-permute-start | bytes 983048 | tf_op jit(solution)/shard_map/ppermute | solution.py:496
  118.4 0.7 collective-permute-start.26
  119.6 2.7 %copy-start.25 = (bf16[1,4,1,32,1280]{4,3,2,1,0:T(8,128)(2,1)S(1)}, bf16[1,4,1,32,1280]{4,3,2,1,0:T(8,128)(2,1)}, u32[]{:S(2)}) copy-start(bf16[1,4,1,32,1280]{4,3,2,1,0:T(8,128)(2,1)} %param.14) | copy-start | bytes 983044
  119.7 2.7 %copy-start.32 = (s32[4]{0:T(128)S(1)}, s32[4]{0:T(128)}, u32[]{:S(2)}) copy-start(s32[4]{0:T(128)} %order_ref.1) | copy-start | bytes 52
  119.7 0.8 collective-permute-start.27
  121.1 46.3 %collective-permute-start.28 = (bf16[128,1280]{1,0:T(8,128)(2,1)S(1)}, bf16[128,1280]{1,0:T(8,128)(2,1)S(1)}, u32[]{:S(2)}, u32[]{:S(2)}) collective-permute-start(bf16[128,1280]{1,0:T(8,128)(2,1)S(1)} %shard_map.126), channel_id=1, source_target_pairs={{24,0},{25,1},{26,2},{27,3},{28,4},{29,5},{30,6},{31,7}} | collective-permute-start | bytes 983048 | tf_op jit(solution)/shard_map/ppermute | solution.py:526
  123.4 7.6 %collective-permute-start.29 = (bf16[1,32,1280]{2,1,0:T(8,128)(2,1)S(1)}, bf16[1,32,1280]{2,1,0:T(8,128)(2,1)S(1)}, u32[]{:S(2)}, u32[]{:S(2)}) collective-permute-start(bf16[1,32,1280]{2,1,0:T(8,128)(2,1)S(1)} %get-tuple-element.101), channel_id=1, source_target_pairs={{0,1},{1,0},{2,3},{3,2},{4,5},{5,4},{6,7},{7,6}} | collective-permute-start | bytes 245768 | tf_op jit(solution)/shard_map/ppermute | solution.py:406
  125.3 6.7 %collective-permute-start.30 = (bf16[1,32,1280]{2,1,0:T(8,128)(2,1)S(1)}, bf16[1,32,1280]{2,1,0:T(8,128)(2,1)S(1)}, u32[]{:S(2)}, u32[]{:S(2)}) collective-permute-start(bf16[1,32,1280]{2,1,0:T(8,128)(2,1)S(1)} %get-tuple-element.102), channel_id=1, source_target_pairs={{0,2},{1,3},{2,0},{3,1},{4,6},{5,7},{6,4},{7,5}} | collective-permute-start | bytes 245768 | tf_op jit(solution)/shard_map/ppermute | solution.py:406
  128.8 6.2 %collective-permute-start.31 = (bf16[1,32,1280]{2,1,0:T(8,128)(2,1)S(1)}, bf16[1,32,1280]{2,1,0:T(8,128)(2,1)S(1)}, u32[]{:S(2)}, u32[]{:S(2)}) collective-permute-start(bf16[1,32,1280]{2,1,0:T(8,128)(2,1)S(1)} %get-tuple-element.103), channel_id=1, source_target_pairs={{0,3},{1,2},{2,1},{3,0},{4,7},{5,6},{6,5},{7,4}} | collective-permute-start | bytes 245768 | tf_op jit(solution)/shard_map/ppermute | solution.py:406
  173.7 6.8 %collective-permute-start.32 = (bf16[128,1280]{1,0:T(8,128)(2,1)S(1)}, bf16[128,1280]{1,0:T(8,128)(2,1)S(1)}, u32[]{:S(2)}, u32[]{:S(2)}) collective-permute-start(bf16[128,1280]{1,0:T(8,128)(2,1)S(1)} %shard_map.128), channel_id=1, source_target_pairs={{0,8},{1,9},{2,10},{3,11},{4,12},{5,13},{6,14},{7,15}} | collective-permute-start | bytes 983048 | tf_op jit(solution)/shard_map/ppermute | solution.py:526
  181.1 0.7 collective-permute-start.33
  182.3 0.7 collective-permute-start.34
  184.0 2.7 %collective-permute-start.35 = (bf16[128,320]{1,0:T(8,128)(2,1)S(1)}, bf16[128,320]{1,0:T(8,128)(2,1)S(1)}, u32[]{:S(2)}, u32[]{:S(2)}) collective-permute-start(bf16[128,320]{1,0:T(8,128)(2,1)S(1)} %get-tuple-element.112), channel_id=1, source_target_pairs={{24,16},{25,17},{26,18},{27,19},{28,20},{29,21},{30,22},{31,23}} | collective-permute-start | bytes 245768 | tf_op jit(solution)/shard_map/ppermute | solution.py:533
  184.6 2.0 collective-permute-start.36
  185.3 38.1 %collective-permute-start.37 = (bf16[128,320]{1,0:T(8,128)(2,1)S(1)}, bf16[128,320]{1,0:T(8,128)(2,1)S(1)}, u32[]{:S(2)}, u32[]{:S(2)}) collective-permute-start(bf16[128,320]{1,0:T(8,128)(2,1)S(1)} %get-tuple-element.110), channel_id=1, source_target_pairs={{24,0},{25,1},{26,2},{27,3},{28,4},{29,5},{30,6},{31,7}} | collective-permute-start | bytes 245768 | tf_op jit(solution)/shard_map/ppermute | solution.py:533
  223.6 3.3 %collective-permute-start.40 = (bf16[1,32,320]{2,1,0:T(8,128)(2,1)S(1)}, bf16[1,32,320]{2,1,0:T(8,128)(2,1)S(1)}, u32[]{:S(2)}, u32[]{:S(2)}) collective-permute-start(bf16[1,32,320]{2,1,0:T(8,128)(2,1)S(1)} %get-tuple-element.121), channel_id=1, source_target_pairs={{0,3},{1,2},{2,1},{3,0},{4,7},{5,6},{6,5},{7,4},{8,11},{9,10},{10,... | collective-permute-start | bytes 61448 | tf_op jit(solution)/shard_map/ppermute | solution.py:406
  223.6 3.9 %collective-permute-start.39 = (bf16[1,32,320]{2,1,0:T(8,128)(2,1)S(1)}, bf16[1,32,320]{2,1,0:T(8,128)(2,1)S(1)}, u32[]{:S(2)}, u32[]{:S(2)}) collective-permute-start(bf16[1,32,320]{2,1,0:T(8,128)(2,1)S(1)} %get-tuple-element.120), channel_id=1, source_target_pairs={{0,2},{1,3},{2,0},{3,1},{4,6},{5,7},{6,4},{7,5},{8,10},{9,11},{10,... | collective-permute-start | bytes 61448 | tf_op jit(solution)/shard_map/ppermute | solution.py:406
  224.1 3.4 %collective-permute-start.38 = (bf16[1,32,320]{2,1,0:T(8,128)(2,1)S(1)}, bf16[1,32,320]{2,1,0:T(8,128)(2,1)S(1)}, u32[]{:S(2)}, u32[]{:S(2)}) collective-permute-start(bf16[1,32,320]{2,1,0:T(8,128)(2,1)S(1)} %get-tuple-element.119), channel_id=1, source_target_pairs={{0,1},{1,0},{2,3},{3,2},{4,5},{5,4},{6,7},{7,6},{8,9},{9,8},{10,11... | collective-permute-start | bytes 61448 | tf_op jit(solution)/shard_map/ppermute | solution.py:406
  (11 other events, 8.4 us)
